TPU v7x, 128 devices: a whole 4x4x4 slice. The times are simulated.
128 devices in a mesh: row: 8 (over x, core), col: 16 (over z, y).
Axes of the slice: x: 4, y: 4, z: 4, core: 2. Of those that a mesh axis runs over, the one named last changes fastest.
Arguments:
- matrix: float32 [8192, 8192], P('row', 'col'), as said below
- start_vectors: float32 [8192, 512], P(('col', 'row')), may hold values from -6 to 6
- interval: float32 [2], replicated, as said below
Outputs:
- ortho_basis: float32 [8192, 512], P(('col', 'row'))
- projected: float32 [512, 512], replicated
- residual: float32 [8192, 512], P(('col', 'row'))
Inputs may be any that keep to these rules, and one draw needn't show every extreme that they name: matrix is exactly symmetric (entry (r, c) equals entry (c, r)); its eigenvalues lie within about -1.45 to 1.45. interval[0] lies in [-1.2, -0.7] and interval[1] in [1.45, 1.9].
All inputs are finite; a program needn't handle non-finite values.
Results may differ from a plain program's by a relative error of at most 0.0003.
Values sent between devices are 32-bit elements.
A program may use at most 128 MiB of HBM per device.

v0:
```python
import functools

import jax
import jax.numpy as jnp
from jax import lax
from jax.experimental import pallas as pl
from jax.experimental.pallas import tpu as pltpu
from jax.sharding import PartitionSpec as P

FILTER_DEG = 3
OUTER = 2
PANEL = 8


def product(left, right, precision=lax.Precision.HIGHEST):
    return jnp.dot(left, right, precision=precision, preferred_element_type=jnp.float32)


def contract(left, right, left_dim, right_dim):
    return lax.dot_general(
        left,
        right,
        (((left_dim,), (right_dim,)), ((), ())),
        precision=lax.Precision.HIGHEST,
        preferred_element_type=jnp.float32,
    )


def factor_panel(panel, first):
    rows = panel.shape[0]
    row_at = lax.broadcasted_iota(jnp.int32, panel.shape, 0)
    pivots = jnp.ones((rows, 1), jnp.float32)
    pivot_at = lax.broadcasted_iota(jnp.int32, (rows, 1), 0)
    for step in range(rows):
        column = panel[:, first + step : first + step + 1]
        pivot = column[step : step + 1, :]
        pivots = jnp.where(pivot_at == step, pivot, pivots)
        if step < rows - 1:
            multiplier = column / pivot
            change = multiplier * panel[step : step + 1, :]
            panel = jnp.where(row_at > step, panel - change, panel)
    return panel * lax.rsqrt(pivots)


def factor_kernel(block, gram_ref, inverse_ref, work, tile):
    order = gram_ref.shape[0]
    work[...] = gram_ref[...]
    at_row = lax.broadcasted_iota(jnp.int32, (order, order), 0)
    at_col = lax.broadcasted_iota(jnp.int32, (order, order), 1)
    inverse_ref[...] = (at_row == at_col).astype(jnp.float32)
    unit = (
        lax.broadcasted_iota(jnp.int32, (block, block), 0)
        == lax.broadcasted_iota(jnp.int32, (block, block), 1)
    ).astype(jnp.float32)
    for start in range(0, order, block):
        stop = start + block
        tile[:, :block] = work[start:stop, start:stop]
        tile[:, block:] = unit
        for first in range(0, block, PANEL):
            last = first + PANEL
            done = factor_panel(tile[first:last, :], first)
            tile[first:last, :] = done
            if last < block:
                tile[last:, :] -= contract(done[:, :block], done, 0, 0)[last:, :]
        small = tile[:, block:]
        solved = product(small, inverse_ref[start:stop, :])
        inverse_ref[start:stop, :] = solved
        if stop < order:
            below = contract(work[stop:, start:stop], small, 1, 1)
            work[stop:, stop:] -= contract(below, below, 1, 1)
            inverse_ref[stop:, :] -= product(below, solved)
    inverse_ref[...] = jnp.where(at_row >= at_col, inverse_ref[...], 0.0)


def inverse_factor(gram_matrix):
    order = gram_matrix.shape[0]
    block = min(128, order)
    return pl.pallas_call(
        functools.partial(factor_kernel, block),
        out_shape=jax.ShapeDtypeStruct((order, order), jnp.float32),
        in_specs=[pl.BlockSpec(memory_space=pltpu.VMEM)],
        out_specs=pl.BlockSpec(memory_space=pltpu.VMEM),
        scratch_shapes=[
            pltpu.VMEM((order, order), jnp.float32),
            pltpu.VMEM((block, 2 * block), jnp.float32),
        ],
        cost_estimate=pl.CostEstimate(flops=2 * order**3, bytes_accessed=8 * order**2, transcendentals=order),
    )(gram_matrix)


def on_device(matrix, start_vectors, interval):
    block_rows = matrix.shape[0]
    slab_rows, vectors = start_vectors.shape
    row_count, col_count = lax.axis_size("row"), lax.axis_size("col")
    total_rows = slab_rows * row_count * col_count
    width = vectors // col_count
    row_index = lax.axis_index("row")
    center = 0.5 * (interval[0] + interval[1])
    half_width = 0.5 * (interval[1] - interval[0])

    strip = lax.all_gather(matrix, "col", axis=1, tiled=True)
    global_rows = row_index * block_rows + lax.iota(jnp.int32, block_rows)
    diagonal = global_rows[:, None] == lax.iota(jnp.int32, total_rows)[None, :]
    shifted = jnp.where(diagonal, strip - center, strip) / half_width

    def apply(group):
        return lax.all_gather(product(shifted, group, lax.Precision.HIGH), "row", axis=0, tiled=True)

    def to_group(slab):
        mine = lax.all_to_all(slab, "col", split_axis=1, concat_axis=0, tiled=True)
        every = lax.all_gather(mine.reshape(col_count, slab_rows, width), "row", axis=1)
        return every.reshape(total_rows, width)

    def to_slab(group):
        parts = group.reshape(col_count, row_count, slab_rows, width)
        mine = lax.dynamic_index_in_dim(parts, row_index, 1, keepdims=False)
        return lax.all_to_all(mine.reshape(col_count * slab_rows, width), "col", split_axis=0, concat_axis=1, tiled=True)

    def filtered(group):
        previous, current = group, apply(group)
        for degree in range(2, FILTER_DEG + 1):
            previous, current = current, 2.0 * apply(current) - previous
        return current

    group = to_group(start_vectors)
    inverses = []

    def normalised(slab):
        for inverse in inverses:
            slab = contract(slab, inverse, 1, 1)
        return slab

    for sweep_index in range(OUTER):
        group = filtered(group)
        slab = normalised(to_slab(group))
        if sweep_index == OUTER - 1:
            mapped = normalised(to_slab(apply(group)))
            pair = jnp.concatenate([slab, mapped], axis=1)
            sums = lax.psum(contract(slab, pair, 0, 0), ("row", "col")) / total_rows
            gram, cross = sums[:, :vectors], sums[:, vectors:]
        else:
            gram = lax.psum(contract(slab, slab, 0, 0), ("row", "col")) / total_rows
        inverses.append(inverse_factor(gram))
    inverse = inverses[-1]
    basis = contract(slab, inverse, 1, 1)
    projected = contract(product(inverse, cross), inverse, 1, 1)
    residual = contract(mapped, inverse, 1, 1) - product(basis, projected)
    return basis, projected, residual


def solution(mesh):
    return jax.shard_map(
        on_device,
        mesh=mesh,
        in_specs=(P("row", "col"), P(("col", "row"), None), P()),
        out_specs=(P(("col", "row"), None), P(), P(("col", "row"), None)),
        check_vma=False,
    )
```

profile of v0, /device:TPU:1, one launch (start us, length us, event | category | flops | bytes accessed | tf_op | source)
XLA Modules:
  0.0 1044.0 jit_solution(5994867720409002756)
XLA Ops:
  8.4 15.2 %all_to_all.73 = f32[16,1,2048]{2,1,0:T(1,128)S(1)} all-to-all(f32[16,1,2048]{2,1,0:T(1,128)S(1)} %reshape.56), channel_id=1, replica_groups=mesh['row'=8,'col'=16] {'col'}, dimensions={0} | all-to-all | bytes 262144 | tf_op jit(solution)/shard_map/all_to_all | solution.py:110
  31.1 26.8 %all-gather.27.cloned.1.call-done = f32[16,512,32]{2,0,1:T(8,128)} async-done(((f32[16,64,32]{2,0,1:T(8,128)}), f32[16,512,32]{2,0,1:T(8,128)}) %all-gather.27.cloned.1.call-update) | async-done | bytes 1048592 | tf_op jit(solution)/shard_map/all_gather | solution.py:111
  57.9 3.2 copy.14
  61.7 194.5 %all-gather.11.cloned.1.call-done = f32[1024,8192]{1,0:T(8,128)} async-done(((f32[1024,512]{1,0:T(8,128)}), f32[1024,8192]{1,0:T(8,128)}) %all-gather.11.cloned.1.call-update) | async-done | bytes 33554448 | tf_op jit(solution)/shard_map/all_gather | solution.py:101
  256.3 23.7 %fusion = f32[1024,8192]{1,0:T(8,128)} fusion(f32[1024,8192]{1,0:T(8,128)} %all-gather.11.cloned.1.call-done, f32[]{:T(128)} %bitcast.1, f32[]{:T(128)} %bitcast, s32[1024]{0:T(1024)S(1)} %iota_add_fusion), kind=kLoop, calls=%fused_computation.1 | loop fusion | flops 33554432 | bytes 67112968 | tf_op jit(solution)/shard_map/div | solution.py:104
  280.0 21.1 %fusion.22 = f32[1024,32]{0,1:T(8,128)} fusion(f32[1024,8192]{1,0:T(8,128)} %fusion, f32[8192,32]{0,1:T(8,128)S(1)} %bitcast.82), kind=kOutput, calls=%fused_computation.37 | convolution fusion | flops 1610612736 | bytes 34734080 | tf_op jit(solution)/shard_map/dot_general | solution.py:16
  301.4 23.2 %all-gather.13.cloned.1.call-done = f32[8192,32]{0,1:T(8,128)} async-done(((f32[1024,32]{0,1:T(8,128)}), f32[8192,32]{0,1:T(8,128)}) %all-gather.13.cloned.1.call-update) | async-done | bytes 1048592 | tf_op jit(solution)/shard_map/all_gather | solution.py:107
  324.6 25.8 %fusion.23 = f32[1024,32]{0,1:T(8,128)} fusion(f32[1024,8192]{1,0:T(8,128)} %fusion, f32[8192,32]{0,1:T(8,128)} %all-gather.13.cloned.1.call-done), kind=kOutput, calls=%fused_computation.38 | convolution fusion | flops 1610612736 | bytes 34734080 | tf_op jit(solution)/shard_map/dot_general | solution.py:16
  350.5 23.1 %all-gather.15.cloned.1.call-done = f32[8192,32]{0,1:T(8,128)} async-done(((f32[1024,32]{0,1:T(8,128)}), f32[8192,32]{0,1:T(8,128)}) %all-gather.15.cloned.1.call-update) | async-done | bytes 1048592 | tf_op jit(solution)/shard_map/all_gather | solution.py:107
  373.6 21.3 %fusion.6 = f32[1024,32]{0,1:T(8,128)} fusion(f32[1024,8192]{1,0:T(8,128)} %fusion, f32[8192,32]{0,1:T(8,128)S(1)} %bitcast.83, f32[8192,32]{0,1:T(8,128)} %all-gather.15.cloned.1.call-done), kind=kOutput, calls=%fused_computation.12 | convolution fusion | flops 1611137024 | bytes 35782656 | tf_op jit(solution)/shard_map/dot_general | solution.py:16
  395.4 22.7 %all-gather.17.cloned.1.call-done = f32[8192,32]{0,1:T(8,128)} async-done(((f32[1024,32]{0,1:T(8,128)}), f32[8192,32]{0,1:T(8,128)}) %all-gather.17.cloned.1.call-update) | async-done | bytes 1048592 | tf_op jit(solution)/shard_map/all_gather | solution.py:107
  419.4 21.1 %fusion.24 = f32[1024,32]{0,1:T(8,128)} fusion(f32[1024,8192]{1,0:T(8,128)} %fusion, f32[8192,32]{0,1:T(8,128)S(1)} %multiply_subtract_fusion.1), kind=kOutput, calls=%fused_computation.39 | convolution fusion | flops 1610612736 | bytes 34734080 | tf_op jit(solution)/shard_map/dot_general | solution.py:16
  440.6 23.1 %all-gather.19.cloned.1.call-done = f32[8192,32]{0,1:T(8,128)} async-done(((f32[1024,32]{0,1:T(8,128)}), f32[8192,32]{0,1:T(8,128)}) %all-gather.19.cloned.1.call-update) | async-done | bytes 1048592 | tf_op jit(solution)/shard_map/all_gather | solution.py:107
  463.7 21.3 %fusion.25 = f32[1024,32]{0,1:T(8,128)} fusion(f32[1024,8192]{1,0:T(8,128)} %fusion, f32[8192,32]{0,1:T(8,128)} %all-gather.19.cloned.1.call-done), kind=kOutput, calls=%fused_computation.40 | convolution fusion | flops 1610612736 | bytes 34734080 | tf_op jit(solution)/shard_map/dot_general | solution.py:16
  485.3 22.9 %all-gather.21.cloned.1.call-done = f32[8192,32]{0,1:T(8,128)} async-done(((f32[1024,32]{0,1:T(8,128)}), f32[8192,32]{0,1:T(8,128)}) %all-gather.21.cloned.1.call-update) | async-done | bytes 1048592 | tf_op jit(solution)/shard_map/all_gather | solution.py:107
  508.2 21.3 %fusion.3 = f32[1024,32]{0,1:T(8,128)} fusion(f32[1024,8192]{1,0:T(8,128)} %fusion, f32[8192,32]{0,1:T(8,128)S(1)} %multiply_subtract_fusion.1, f32[8192,32]{0,1:T(8,128)} %all-gather.21.cloned.1.call-done), kind=kOutput, calls=%fused_computation.8 | convolution fusion | flops 1611137024 | bytes 35782656 | tf_op jit(solution)/shard_map/dot_general | solution.py:16
  533.8 13.3 %all_to_all.74 = f32[16,1,2048]{2,1,0:T(1,128)S(1)} all-to-all(f32[16,1,2048]{2,1,0:T(1,128)S(1)} %reshape.60), channel_id=1, replica_groups=mesh['row'=8,'col'=16] {'col'}, dimensions={0} | all-to-all | bytes 262144 | tf_op jit(solution)/shard_map/all_to_all | solution.py:117
  550.2 2.5 all-gather.23.cloned.1.call-done
  554.0 21.1 %fusion.28 = f32[1024,32]{0,1:T(8,128)} fusion(f32[1024,8192]{1,0:T(8,128)} %fusion, f32[8192,32]{0,1:T(8,128)S(1)} %multiply_subtract_fusion), kind=kOutput, calls=%fused_computation.43 | convolution fusion | flops 1610612736 | bytes 34734080 | tf_op jit(solution)/shard_map/dot_general | solution.py:16
  577.1 7.1 all-to-all-start.1
  584.3 123.5 %all-reduce.3.cloned.1.call-done = f32[512,512]{1,0:T(8,128)} async-done(((f32[512,512]{1,0:T(8,128)}), f32[512,512]{1,0:T(8,128)}) %all-reduce.3.cloned.1.call-update) | async-done | bytes 1048592 | tf_op jit(solution)/shard_map/psum | solution.py:142
  710.0 69.7 %shard_map.58 = f32[512,512]{1,0:T(8,128)} custom-call(f32[512,512]{1,0:T(8,128)} %broadcast_multiply_fusion.1.gram_ref), custom_call_target="tpu_custom_call" | custom-call | flops 268435456 | bytes 2097152 | tf_op jit(solution)/shard_map/pallas_call | solution.py:78
  783.9 4.7 all-to-all-start.3
  788.8 2.4 fusion.27
  791.2 4.2 all-to-all-done.3
  796.4 2.4 fusion.29
  798.8 3.2 fusion.11
  802.0 150.0 %all-reduce.5.cloned.1.call-done = f32[512,1024]{1,0:T(8,128)} async-done(((f32[512,1024]{1,0:T(8,128)}), f32[512,1024]{1,0:T(8,128)}) %all-reduce.5.cloned.1.call-update) | async-done | bytes 2097168 | tf_op jit(solution)/shard_map/psum | solution.py:139
  954.8 69.9 %shard_map.59 = f32[512,512]{1,0:T(8,128)} custom-call(f32[512,512]{1,0:T(8,128)} %slice.18.gram_ref), custom_call_target="tpu_custom_call" | custom-call | flops 268435456 | bytes 2097152 | tf_op jit(solution)/shard_map/pallas_call | solution.py:78
  1027.1 3.3 fusion.1
  1030.3 2.3 fusion.30
  1032.7 3.1 fusion.31
  (68 shorter events, 34.0 us)
Async XLA Ops:
  7.2 50.7 %all-gather.27.cloned.1.call-start = ((), (), s32[]{:S(2)}) async-start(), calls=%async_computation.14 | async-start | bytes 4718592 | tf_op jit(solution)/shard_map/all_gather | solution.py:111
  26.4 229.9 %all-gather.11.cloned.1.call-start = ((), (), s32[]{:S(2)}) async-start(), calls=%async_computation.4 | async-start | bytes 35651584 | tf_op jit(solution)/shard_map/all_gather | solution.py:101
  27.1 297.5 %all-gather.13.cloned.1.call-start = ((), (), s32[]{:S(2)}) async-start(), calls=%async_computation.5 | async-start | bytes 1179648 | tf_op jit(solution)/shard_map/all_gather | solution.py:107
  301.1 72.5 %all-gather.15.cloned.1.call-start = ((), (), s32[]{:S(2)}) async-start(), calls=%async_computation.6 | async-start | bytes 1179648 | tf_op jit(solution)/shard_map/all_gather | solution.py:107
  324.6 93.5 %copy-start.1 = (f32[8192,32]{0,1:T(8,128)S(1)}, f32[8192,32]{0,1:T(8,128)}, u32[]{:S(2)}) copy-start(f32[8192,32]{0,1:T(8,128)} %all-gather.13.cloned.1.call-done) | copy-start | bytes 3145732
  350.5 67.6 %all-gather.17.cloned.1.call-start = ((), (), s32[]{:S(2)}) async-start(), calls=%async_computation.7 | async-start | bytes 1179648 | tf_op jit(solution)/shard_map/all_gather | solution.py:107
  395.0 68.8 %all-gather.19.cloned.1.call-start = ((), (), s32[]{:S(2)}) async-start(), calls=%async_computation.8 | async-start | bytes 1179648 | tf_op jit(solution)/shard_map/all_gather | solution.py:107
  440.6 67.6 %all-gather.21.cloned.1.call-start = ((), (), s32[]{:S(2)}) async-start(), calls=%async_computation.9 | async-start | bytes 1179648 | tf_op jit(solution)/shard_map/all_gather | solution.py:107
  485.0 67.7 %copy-start = (f32[8192,32]{0,1:T(8,128)S(1)}, f32[8192,32]{0,1:T(8,128)}, u32[]{:S(2)}) copy-start(f32[8192,32]{0,1:T(8,128)} %all-gather.19.cloned.1.call-done) | copy-start | bytes 3145732
  485.1 67.6 %all-gather.23.cloned.1.call-start = ((), (), s32[]{:S(2)}) async-start(), calls=%async_computation.10 | async-start | bytes 1179648 | tf_op jit(solution)/shard_map/all_gather | solution.py:107
  529.6 178.2 %all-reduce.3.cloned.1.call-start = ((), (), s32[]{:S(2)}) async-start(), calls=%async_computation.11 | async-start | bytes 2097152 | tf_op jit(solution)/shard_map/psum | solution.py:142
  550.2 230.5 %all-gather.25.cloned.1.call-start = ((), (), s32[]{:S(2)}) async-start(), calls=%async_computation.12 | async-start | bytes 1179648 | tf_op jit(solution)/shard_map/all_gather | solution.py:107
  577.1 202.5 %all-to-all-start.1 = ((f32[16,1,2048]{2,1,0:T(1,128)}), f32[16,1,2048]{2,1,0:T(1,128)S(1)}, u32[]{:S(2)}, u32[]{:S(2)}) async-start(f32[16,1,2048]{2,1,0:T(1,128)} %reshape.58), calls=%async_computation.1 | async-start | bytes 262144 | tf_op jit(solution)/shard_map/all_to_all | solution.py:117
  783.9 11.5 %all-to-all-start.3 = ((f32[16,1,2048]{2,1,0:T(1,128)}), f32[16,1,2048]{2,1,0:T(1,128)S(1)}, u32[]{:S(2)}, u32[]{:S(2)}) async-start(f32[16,1,2048]{2,1,0:T(1,128)} %reshape.62), calls=%async_computation.3 | async-start | bytes 262144 | tf_op jit(solution)/shard_map/all_to_all | solution.py:117
  788.6 163.4 %all-reduce.5.cloned.1.call-start = ((), (), s32[]{:S(2)}) async-start(), calls=%async_computation.13 | async-start | bytes 4194304 | tf_op jit(solution)/shard_map/psum | solution.py:139
  1032.7 4.6 copy-start.3
  1035.8 1.4 copy-start.2
Sparse Core Ops, SparseCore 0:
  26.5 31.3 all-gather.26
  60.0 196.2 all-gather.10
  301.3 23.3 all-gather.12
  350.6 22.9 all-gather.14
  395.1 22.9 all-gather.16
  440.7 22.9 all-gather.18
  485.2 22.9 all-gather.20
  529.7 22.9 all-gather.22
  558.1 149.5 all-reduce.2
  709.8 22.6 all-gather.24
  802.1 149.8 all-reduce.4
where the time goes:
time: 1050 us; the launch traced here: 1040 us
  waiting for transfers between devices  617 us (59%)
  matrix products  175 us (17%)
  Pallas kernels  140 us (13%)
  other arithmetic  34.1 us (3%)
  blocking collectives  28.6 us (3%)
  local copies, waits for them, and re-layouts  18.8 us (2%)
  between operations  16.9 us (2%)
  starting transfers between devices  13.2 us (1%)
    all_gather x1, waiting for transfers between devices, on_device(): strip = lax.all_gather(matrix, 'col', axis=1, tiled=True)  195 us
    dot_general x9, matrix products, product(): jnp.dot(left, right, precision=precision, preferred_element_type=jnp.floa...  158 us
    psum x1, waiting for transfers between devices, on_device(): sums = lax.psum(contract(slab, pair, 0, 0), ('row', 'col')) / total_rows  150 us
    pallas_call x2, Pallas kernels, inverse_factor(): pl.pallas_call(functools.partial(factor_kernel, block), out_shape=jax.Sha...  140 us
    psum x1, waiting for transfers between devices, on_device(): gram = lax.psum(contract(slab, slab, 0, 0), ('row', 'col')) / total_rows  123 us
    all_gather x7, waiting for transfers between devices, apply(): lax.all_gather(product(shifted, group, lax.Precision.HIGH), 'row', axis=0...  118 us
    all_gather x1, waiting for transfers between devices, to_group(): lax.all_gather(mine.reshape(col_count, slab_rows, width), 'row', axis=1)  26.8 us
    div x1, other arithmetic, on_device(): shifted = jnp.where(diagonal, strip - center, strip) / half_width  23.7 us
  transfers between devices with their start and end apart: 13, of which 11 were waited for; matrix products, arithmetic and copies ran while one was open for 4% of the time, Pallas kernels for 7%

commit v1 on v0

--- a/solution.py
+++ b/solution.py
@@ -10,6 +10,8 @@
 FILTER_DEG = 3
 OUTER = 2
 PANEL = 8
+MESH = pl.DeviceIdType.MESH
+CHUNK = 128
 
 
 def product(left, right, precision=lax.Precision.HIGHEST):
@@ -88,60 +90,427 @@
     )(gram_matrix)
 
 
+class Copies:
+    def __init__(self, send, recv):
+        self.send, self.recv, self.used = send, recv, 0
+
+    def reserve(self, count):
+        first = self.used
+        self.used += count
+        return first
+
+    def make(self, source, target, slot, device):
+        return pltpu.make_async_remote_copy(
+            src_ref=source,
+            dst_ref=target,
+            send_sem=self.send.at[slot],
+            recv_sem=self.recv.at[slot],
+            device_id=device,
+            device_id_type=MESH,
+        )
+
+
+class Scatter:
+    def __init__(self, copies, slot, place, ring, part, land):
+        self.place, self.part, self.land = place, part, land
+        left, right = ring
+        ahead, behind, across = (place + 1) % 4, (place + 3) % 4, (place + 2) % 4
+        self.ahead, self.behind = ahead, behind
+        plan = (
+            (part(across, 0), right),
+            (part(across, 1), left),
+            (part(ahead, 1), right),
+            (part(behind, 0), left),
+            (part(ahead, 0), right),
+            (part(behind, 1), left),
+        )
+        self.copies = [
+            copies.make(source, land(i), slot + i, device) for i, (source, device) in enumerate(plan)
+        ]
+
+    def start(self):
+        for copy in self.copies[:4]:
+            copy.start()
+
+    def relay(self):
+        for first, half, target in ((0, 0, self.ahead), (1, 1, self.behind)):
+            self.copies[first].wait_recv()
+            mine = self.part(target, half)
+            mine[...] += self.land(first)[...]
+            self.copies[4 + first].start()
+
+    def finish(self):
+        for copy in self.copies[2:]:
+            copy.wait_recv()
+        for half, terms in ((0, (3, 4)), (1, (2, 5))):
+            mine = self.part(self.place, half)
+            mine[...] += self.land(terms[0])[...] + self.land(terms[1])[...]
+        for copy in self.copies:
+            copy.wait_send()
+
+
+class Gather:
+    def __init__(self, copies, slot, place, ring, part):
+        left, right = ring
+        ahead, behind = (place + 1) % 4, (place + 3) % 4
+        self.copies = [
+            copies.make(part(place, None), part(place, None), slot, right),
+            copies.make(part(place, None), part(place, None), slot + 1, left),
+            copies.make(part(behind, 0), part(behind, 0), slot + 2, right),
+            copies.make(part(ahead, 1), part(ahead, 1), slot + 3, left),
+        ]
+
+    def start(self):
+        for copy in self.copies[:2]:
+            copy.start()
+
+    def forward(self):
+        for first in range(2):
+            self.copies[first].wait_recv()
+            self.copies[2 + first].start()
+
+    def finish(self):
+        for copy in self.copies[2:]:
+            copy.wait_recv()
+        for copy in self.copies:
+            copy.wait_send()
+
+
+def split(value):
+    high = value.astype(jnp.bfloat16)
+    return high, (value - high.astype(jnp.float32)).astype(jnp.bfloat16)
+
+
+def three_pass(left, right, dims):
+    def one(a, b):
+        return lax.dot_general(a, b, (dims, ((), ())), preferred_element_type=jnp.float32)
+
+    return one(left[0], right[0]) + (one(left[0], right[1]) + one(left[1], right[0]))
+
+
+def filter_kernel(
+    scale_ref, block_ref, start_ref, first_ref, last_ref, image_ref,
+    other, high, low, rows, row_parts, cols, col_parts, vec_high, vec_low,
+    land_big, land_small, land_col, row_prev, col_prev, first_part,
+    start_land, first_land, last_land, image_land, send, recv,
+):
+    r, c = lax.axis_index("row"), lax.axis_index("col")
+    core, x, y, z = r % 2, r // 2, c % 4, c // 4
+    copies = Copies(send, recv)
+
+    def device(x, core, y, z):
+        return (2 * x + core, 4 * z + y)
+
+    mate = device(x, 1 - core, y, z)
+    ring_x = device((x + 3) % 4, core, y, z), device((x + 1) % 4, core, y, z)
+    ring_y = device(x, core, (y + 3) % 4, z), device(x, core, (y + 1) % 4, z)
+    ring_z = device(x, core, y, (z + 3) % 4), device(x, core, y, (z + 1) % 4)
+    crossed = x != z
+
+    barrier = pltpu.get_barrier_semaphore()
+
+    def greet(who):
+        pl.semaphore_signal(barrier, inc=1, device_id=who, device_id_type=MESH)
+
+    for who in (mate, *ring_x, *ring_y, *ring_z):
+        greet(who)
+
+    @pl.when(crossed)
+    def _():
+        greet(device(z, core, y, x))
+        greet(device(z, 1 - core, y, x))
+
+    pl.semaphore_wait(barrier, jnp.where(crossed, 9, 7))
+
+    block_rows, block_cols = block_ref.shape
+    slab = start_ref.shape[0]
+    width = start_ref.shape[1] // 2
+    mine_cols = pl.ds(pl.multiple_of(core * width, width), width)
+    mate_cols = pl.ds(pl.multiple_of((1 - core) * width, width), width)
+
+    start_copy = copies.make(start_ref.at[:, mate_cols], start_land, copies.reserve(1), mate)
+    start_copy.start()
+    block_copy = copies.make(block_ref, other, copies.reserve(1), mate)
+    block_copy.start()
+
+    center, inverse_width = scale_ref[0], scale_ref[1]
+
+    def prepare(source, which):
+        base = which * block_rows
+        step = 256
+
+        @pl.loop(0, block_rows // step)
+        def _(i):
+            at = pl.multiple_of(i * step, step)
+            value = source[pl.ds(at, step), :]
+            row = lax.broadcasted_iota(jnp.int32, value.shape, 0) + (2 * x * block_rows + base + at)
+            col = lax.broadcasted_iota(jnp.int32, value.shape, 1) + c * block_cols
+            value = jnp.where(row == col, value - center, value) * inverse_width
+            big, small = split(value)
+            to = pl.ds(pl.multiple_of(base + at, step), step)
+            high[to, :] = big
+            low[to, :] = small
+
+    prepare(block_ref, core)
+
+    start_copy.wait_recv()
+    half = width // 2
+    own = start_ref[:, mine_cols]
+    theirs = start_land[...]
+    lower = jnp.where(core == 0, own, theirs)
+    upper = jnp.where(core == 0, theirs, own)
+    piece = jnp.concatenate([lower, upper], axis=0).T
+    cols[x] = piece
+    col_prev[...] = piece
+    row_prev[...] = jnp.zeros_like(row_prev)
+    start_copy.wait_send()
+
+    def col_slice(ref):
+        def part(t, side):
+            if side is None:
+                return ref.at[t]
+            return ref.at[t, pl.ds(side * half, half), :]
+        return part
+
+    def plane_slice(ref, colour, axis):
+        def part(t, side):
+            size = half if side is None else half // 2
+            at = pl.ds(colour * half + (0 if side is None else side * size), size)
+            return ref.at[:, t, at, :] if axis == "z" else ref.at[t, :, at, :]
+        return part
+
+    def line_slice(ref, colour, axis):
+        def part(t, side):
+            size = half if side is None else half // 2
+            at = pl.ds(colour * half + (0 if side is None else side * size), size)
+            return ref.at[y, t, at, :] if axis == "z" else ref.at[t, z, at, :]
+        return part
+
+    places = {"y": y, "z": z}
+    rings = {"y": ring_y, "z": ring_z}
+    orders = (("z", "y"), ("y", "z"))
+
+    scatter_slots = [[copies.reserve(6) for _ in range(2)] for _ in range(2)]
+    gather_slots = [[copies.reserve(4) for _ in range(2)] for _ in range(2)]
+    col_slots = copies.reserve(6), copies.reserve(4)
+
+    def scatter_stage(colour, stage):
+        axis = orders[colour][stage]
+        ref_slice = (plane_slice if stage == 0 else line_slice)(row_parts, colour, axis)
+        land = (lambda i: land_big.at[colour, i]) if stage == 0 else (lambda i: land_small.at[colour, i])
+        return Scatter(copies, scatter_slots[colour][stage], places[axis], rings[axis], ref_slice, land)
+
+    def gather_stage(colour, stage):
+        axis = orders[colour][1 - stage]
+        ref_slice = (line_slice if stage == 0 else plane_slice)(rows, colour, axis)
+        return Gather(copies, gather_slots[colour][stage], places[axis], rings[axis], ref_slice)
+
+    col_gather = Gather(copies, col_slots[1], x, ring_x, col_slice(cols))
+    col_scatter = Scatter(copies, col_slots[0], x, ring_x, col_slice(col_parts), lambda i: land_col.at[i])
+
+    col_gather.start()
+    col_gather.forward()
+    col_gather.finish()
+
+    block_copy.wait_recv()
+    prepare(other, 1 - core)
+    block_copy.wait_send()
+
+    def to_rows():
+        for q in range(4):
+            big, small = split(cols[q])
+            vec_high[:, q * CHUNK : (q + 1) * CHUNK] = big
+            vec_low[:, q * CHUNK : (q + 1) * CHUNK] = small
+
+        @pl.loop(0, 8)
+        def _(i):
+            at = pl.ds(pl.multiple_of(i * 256, 256), 256)
+            out = three_pass((vec_high[...], vec_low[...]), (high[at, :], low[at, :]), ((1,), (1,)))
+            row_parts[i // 2, 2 * (i % 2)] = out[:, :CHUNK]
+            row_parts[i // 2, 2 * (i % 2) + 1] = out[:, CHUNK:]
+
+        stages = [scatter_stage(0, 0), scatter_stage(1, 0)]
+        for stage in stages:
+            stage.start()
+        for stage in stages:
+            stage.relay()
+        seconds = [scatter_stage(0, 1), scatter_stage(1, 1)]
+        for stage, second in zip(stages, seconds):
+            stage.finish()
+            second.start()
+        for second in seconds:
+            second.relay()
+        return seconds
+
+    def sweep(step, carry):
+        factor = jnp.where(step == 0, 1.0, 2.0)
+        weight = jnp.where(step == 0, 0.0, 1.0)
+        seconds = to_rows()
+        gathers = []
+        for colour, second in enumerate(seconds):
+            second.finish()
+            at = pl.ds(colour * half, half)
+            value = factor * row_parts[y, z, at, :] - weight * row_prev[at, :]
+            rows[y, z, at, :] = value
+            row_prev[at, :] = value
+            first = gather_stage(colour, 0)
+            first.start()
+            gathers.append(first)
+
+        @pl.when(step == 1)
+        def _():
+            first_part[...] = row_prev[...]
+
+        for first in gathers:
+            first.forward()
+        lasts = []
+        for colour, first in enumerate(gathers):
+            first.finish()
+            last = gather_stage(colour, 1)
+            last.start()
+            lasts.append(last)
+        for last in lasts:
+            last.forward()
+        for last in lasts:
+            last.finish()
+
+        for q in range(4):
+            col_parts[q] = jnp.zeros((width, CHUNK), jnp.float32)
+
+        @pl.loop(0, 8)
+        def _(i):
+            at = pl.ds(pl.multiple_of(i * 256, 256), 256)
+            vec = jnp.concatenate([rows[i // 2, 2 * (i % 2)], rows[i // 2, 2 * (i % 2) + 1]], axis=1)
+            out = three_pass(split(vec), (high[at, :], low[at, :]), ((1,), (0,)))
+            for q in range(4):
+                col_parts[q] += out[:, q * CHUNK : (q + 1) * CHUNK]
+
+        col_scatter.start()
+        col_scatter.relay()
+        col_scatter.finish()
+        again = jnp.where(step == 1, 1.0, 2.0)
+        minus = jnp.where(step == 1, 0.0, 1.0)
+        value = again * col_parts[x] - minus * col_prev[...]
+        cols[x] = value
+        col_prev[...] = value
+        col_gather.start()
+        col_gather.forward()
+        col_gather.finish()
+        return carry
+
+    lax.fori_loop(0, 3, sweep, 0)
+    for second in to_rows():
+        second.finish()
+
+    def trade(piece, land, out_ref):
+        turned = piece.T
+        land[1] = turned
+        copy = copies.make(
+            land.at[1, pl.ds(pl.multiple_of((1 - core) * slab, slab), slab), :],
+            land.at[0, pl.ds(pl.multiple_of((1 - core) * slab, slab), slab), :],
+            copies.reserve(1),
+            mate,
+        )
+        copy.start()
+        return copy
+
+    first_copy = trade(first_part[...], first_land, first_ref)
+    last_copy = trade(col_prev[...], last_land, last_ref)
+
+    image_land[2, :, :] = row_parts[y, z].T
+    image_slots = copies.reserve(2)
+
+    same = copies.make(
+        image_land.at[2, pl.ds(pl.multiple_of(core * slab, slab), slab), :],
+        image_land.at[0, pl.ds(0, slab), :],
+        image_slots,
+        device(z, core, y, x),
+    )
+    cross = copies.make(
+        image_land.at[2, pl.ds(pl.multiple_of((1 - core) * slab, slab), slab), :],
+        image_land.at[1, pl.ds(0, slab), :],
+        image_slots + 1,
+        device(z, 1 - core, y, x),
+    )
+    cross.start()
+
+    @pl.when(crossed)
+    def _():
+        same.start()
+        same.wait()
+
+    @pl.when(jnp.logical_not(crossed))
+    def _():
+        image_land[0, pl.ds(0, slab), :] = image_land[2, pl.ds(pl.multiple_of(core * slab, slab), slab), :]
+
+    keep = pl.ds(pl.multiple_of(core * slab, slab), slab)
+    for copy, land, out_ref in ((first_copy, first_land, first_ref), (last_copy, last_land, last_ref)):
+        copy.wait()
+        out_ref[:, mine_cols] = land[1, keep, :]
+        out_ref[:, mate_cols] = land[0, keep, :]
+    cross.wait()
+    image_ref[:, mine_cols] = image_land[0, pl.ds(0, slab), :]
+    image_ref[:, mate_cols] = image_land[1, pl.ds(0, slab), :]
+
+
+def filtered_blocks(matrix, start_vectors, scale):
+    block_rows, block_cols = matrix.shape
+    slab, vectors = start_vectors.shape
+    width = vectors // 2
+    half = width // 2
+    f32, bf16 = jnp.float32, jnp.bfloat16
+    vmem = pl.BlockSpec(memory_space=pltpu.VMEM)
+    return pl.pallas_call(
+        filter_kernel,
+        out_shape=[jax.ShapeDtypeStruct((slab, vectors), f32)] * 3,
+        in_specs=[pl.BlockSpec(memory_space=pltpu.SMEM), vmem, vmem],
+        out_specs=[vmem] * 3,
+        scratch_shapes=[
+            pltpu.VMEM((block_rows, block_cols), f32),
+            pltpu.VMEM((2 * block_rows, block_cols), bf16),
+            pltpu.VMEM((2 * block_rows, block_cols), bf16),
+            pltpu.VMEM((4, 4, width, CHUNK), f32),
+            pltpu.VMEM((4, 4, width, CHUNK), f32),
+            pltpu.VMEM((4, width, CHUNK), f32),
+            pltpu.VMEM((4, width, CHUNK), f32),
+            pltpu.VMEM((width, block_cols), bf16),
+            pltpu.VMEM((width, block_cols), bf16),
+            pltpu.VMEM((2, 6, 4, half // 2, CHUNK), f32),
+            pltpu.VMEM((2, 6, half // 2, CHUNK), f32),
+            pltpu.VMEM((6, half, CHUNK), f32),
+            pltpu.VMEM((width, CHUNK), f32),
+            pltpu.VMEM((width, CHUNK), f32),
+            pltpu.VMEM((width, CHUNK), f32),
+            pltpu.VMEM((slab, width), f32),
+            pltpu.VMEM((2, CHUNK, width), f32),
+            pltpu.VMEM((2, CHUNK, width), f32),
+            pltpu.VMEM((3, CHUNK, width), f32),
+            pltpu.SemaphoreType.DMA((64,)),
+            pltpu.SemaphoreType.DMA((64,)),
+        ],
+        compiler_params=pltpu.CompilerParams(
+            collective_id=0, has_side_effects=True, vmem_limit_bytes=40 * 2**20
+        ),
+        cost_estimate=pl.CostEstimate(flops=10**10, bytes_accessed=4 * 10**6, transcendentals=0),
+    )(scale, matrix, start_vectors)
+
+
 def on_device(matrix, start_vectors, interval):
-    block_rows = matrix.shape[0]
     slab_rows, vectors = start_vectors.shape
-    row_count, col_count = lax.axis_size("row"), lax.axis_size("col")
-    total_rows = slab_rows * row_count * col_count
-    width = vectors // col_count
-    row_index = lax.axis_index("row")
+    total_rows = slab_rows * lax.axis_size("row") * lax.axis_size("col")
     center = 0.5 * (interval[0] + interval[1])
     half_width = 0.5 * (interval[1] - interval[0])
-
-    strip = lax.all_gather(matrix, "col", axis=1, tiled=True)
-    global_rows = row_index * block_rows + lax.iota(jnp.int32, block_rows)
-    diagonal = global_rows[:, None] == lax.iota(jnp.int32, total_rows)[None, :]
-    shifted = jnp.where(diagonal, strip - center, strip) / half_width
-
-    def apply(group):
-        return lax.all_gather(product(shifted, group, lax.Precision.HIGH), "row", axis=0, tiled=True)
-
-    def to_group(slab):
-        mine = lax.all_to_all(slab, "col", split_axis=1, concat_axis=0, tiled=True)
-        every = lax.all_gather(mine.reshape(col_count, slab_rows, width), "row", axis=1)
-        return every.reshape(total_rows, width)
-
-    def to_slab(group):
-        parts = group.reshape(col_count, row_count, slab_rows, width)
-        mine = lax.dynamic_index_in_dim(parts, row_index, 1, keepdims=False)
-        return lax.all_to_all(mine.reshape(col_count * slab_rows, width), "col", split_axis=0, concat_axis=1, tiled=True)
-
-    def filtered(group):
-        previous, current = group, apply(group)
-        for degree in range(2, FILTER_DEG + 1):
-            previous, current = current, 2.0 * apply(current) - previous
-        return current
-
-    group = to_group(start_vectors)
-    inverses = []
-
-    def normalised(slab):
-        for inverse in inverses:
-            slab = contract(slab, inverse, 1, 1)
-        return slab
-
-    for sweep_index in range(OUTER):
-        group = filtered(group)
-        slab = normalised(to_slab(group))
-        if sweep_index == OUTER - 1:
-            mapped = normalised(to_slab(apply(group)))
-            pair = jnp.concatenate([slab, mapped], axis=1)
-            sums = lax.psum(contract(slab, pair, 0, 0), ("row", "col")) / total_rows
-            gram, cross = sums[:, :vectors], sums[:, vectors:]
-        else:
-            gram = lax.psum(contract(slab, slab, 0, 0), ("row", "col")) / total_rows
-        inverses.append(inverse_factor(gram))
-    inverse = inverses[-1]
+    scale = jnp.stack([center, 1.0 / half_width])
+    early, slab, mapped = filtered_blocks(matrix, start_vectors, scale)
+
+    gram = lax.psum(contract(early, early, 0, 0), ("row", "col")) / total_rows
+    before = inverse_factor(gram)
+    slab = contract(slab, before, 1, 1)
+    mapped = contract(mapped, before, 1, 1)
+    pair = jnp.concatenate([slab, mapped], axis=1)
+    sums = lax.psum(contract(slab, pair, 0, 0), ("row", "col")) / total_rows
+    gram, cross = sums[:, :vectors], sums[:, vectors:]
+    inverse = inverse_factor(gram)
     basis = contract(slab, inverse, 1, 1)
     projected = contract(product(inverse, cross), inverse, 1, 1)
     residual = contract(mapped, inverse, 1, 1) - product(basis, projected)

time: 1050 us -> 707 us (0.67)
  waiting for transfers between devices: 617 us -> 304 us
  Pallas kernels: 140 us -> 355 us
  matrix products: 175 us -> 18.5 us
  other arithmetic: 34.1 us -> 4.13 us
  blocking collectives: 28.6 us -> 0 us
  local copies, waits for them, and re-layouts: 18.8 us -> 4.89 us
  starting transfers between devices: 13.2 us -> 0.54 us
    all_gather x9 -> x0, waiting for transfers between devices: 339 us -> none  [the longest x1 195 us: on_device(): strip = lax.all_gather(matrix, 'col', axis=1, tiled=True)]
    pallas_call x0 -> x1, Pallas kernels: none -> 215 us  [filtered_blocks(): pl.pallas_call(filter_kernel, out_shape=[jax.ShapeDtypeStruct((slab, vect...]
    dot_general x9 -> x2, matrix products: 158 us -> 4.57 us  [product(): jnp.dot(left, right, precision=precision, preferred_element_type=jnp.floa...]
    psum x1, waiting for transfers between devices: 123 us -> 153 us  [on_device(): gram = lax.psum(contract(early, early, 0, 0), ('row', 'col')) / total_rows]
    all_to_all x2 -> x0, blocking collectives: 28.6 us -> none  [the longest x1 15.2 us: to_group(): mine = lax.all_to_all(slab, 'col', split_axis=1, concat_axis=0, tiled=True)]
    div x2 -> x1, other arithmetic: 26 us -> 2.29 us  [on_device(): gram = lax.psum(contract(early, early, 0, 0), ('row', 'col')) / total_rows]
    all_to_all x2 -> x0, starting transfers between devices: 11.8 us -> none  [to_slab(): lax.all_to_all(mine.reshape(col_count * slab_rows, width), 'col', split_a...]
  transfers between devices with their start and end apart: 13 -> 2, of which waited for: 11 -> 2; matrix products, arithmetic and copies ran while one was open for 4% -> 0% of each run, Pallas kernels for 7% -> 0%
where the time goes in v1:
time: 707 us; the launch traced here: 704 us
  Pallas kernels  355 us (50%)
  waiting for transfers between devices  304 us (43%)
  matrix products  18.5 us (3%)
  between operations  17.2 us (2%)
    pallas_call x1, Pallas kernels, filtered_blocks(): pl.pallas_call(filter_kernel, out_shape=[jax.ShapeDtypeStruct((slab, vect...  215 us
    psum x1, waiting for transfers between devices, on_device(): gram = lax.psum(contract(early, early, 0, 0), ('row', 'col')) / total_rows  153 us
    psum x1, waiting for transfers between devices, on_device(): sums = lax.psum(contract(slab, pair, 0, 0), ('row', 'col')) / total_rows  151 us
    pallas_call x2, Pallas kernels, inverse_factor(): pl.pallas_call(functools.partial(factor_kernel, block), out_shape=jax.Sha...  140 us
  transfers between devices with their start and end apart: 2, of which 2 were waited for; matrix products, arithmetic and copies ran while one was open for 0% of the time, Pallas kernels for 0%

profile of v1, /device:TPU:1, one launch (start us, length us, event | category | flops | bytes accessed | tf_op | source)
XLA Modules:
  0.0 703.7 jit_solution(13345812773060612252)
XLA Ops:
  7.2 0.0 all-reduce.3.cloned.1.call-start
  7.2 1.3 fusion.7
  11.2 0.1 pad_maximum_fusion.scale_ref
  11.2 0.0 copy-start
  11.2 1.6 copy-done
  12.8 0.0 copy-start.1
  12.8 0.9 copy-done.1
  13.7 215.2 %shard_map.58 = (f32[64,512]{1,0:T(8,128)S(1)}, f32[64,512]{1,0:T(8,128)S(1)}, f32[64,512]{1,0:T(8,128)S(1)}) custom-call(f32[2]{0:T(128)S(1)} %pad_maximum_fusion.scale_ref, f32[1024,512]{1,0:T(8,128)S(1)} %copy-done, f32[64,512]{1,0:T(8,128)S(1)} %copy-done.1), custom_call_target="tpu_custom_call" | custom-call | flops 10000000000 | bytes 4000000 | tf_op jit(solution)/shard_map/pallas_call | solution.py:463
  228.9 2.0 fusion.8
  230.9 0.0 all-reduce.3.cloned.1.call-update
  231.0 0.5 all-reduce.5.cloned.1.call-start
  231.5 152.9 %all-reduce.3.cloned.1.call-done = f32[512,512]{1,0:T(8,128)} async-done(((f32[512,512]{1,0:T(8,128)}), f32[512,512]{1,0:T(8,128)}) %all-reduce.3.cloned.1.call-update) | async-done | bytes 1048592 | tf_op jit(solution)/shard_map/psum | solution.py:506
  384.4 2.3 broadcast_multiply_fusion.1.gram_ref
  386.7 69.7 %shard_map.59 = f32[512,512]{1,0:T(8,128)} custom-call(f32[512,512]{1,0:T(8,128)} %broadcast_multiply_fusion.1.gram_ref), custom_call_target="tpu_custom_call" | custom-call | flops 268435456 | bytes 2097152 | tf_op jit(solution)/shard_map/pallas_call | solution.py:80
  456.3 2.3 fusion.10
  458.7 2.3 fusion.9
  461.0 3.2 fusion.2
  464.1 0.0 all-reduce.5.cloned.1.call-update
  464.2 150.7 %all-reduce.5.cloned.1.call-done = f32[512,1024]{1,0:T(8,128)} async-done(((f32[512,1024]{1,0:T(8,128)}), f32[512,1024]{1,0:T(8,128)}) %all-reduce.5.cloned.1.call-update) | async-done | bytes 2097168 | tf_op jit(solution)/shard_map/psum | solution.py:511
  614.9 1.8 broadcast_multiply_fusion
  616.7 1.1 slice.18.gram_ref
  617.7 69.9 %shard_map.60 = f32[512,512]{1,0:T(8,128)} custom-call(f32[512,512]{1,0:T(8,128)} %slice.18.gram_ref), custom_call_target="tpu_custom_call" | custom-call | flops 268435456 | bytes 2097152 | tf_op jit(solution)/shard_map/pallas_call | solution.py:80
  687.7 0.0 copy-start.2
  687.7 3.2 fusion
  690.8 0.0 copy-done.2
  690.8 1.1 fusion.11
  692.0 1.1 fusion.13
  693.1 1.9 fusion.12
  695.0 0.0 copy-done.4
  695.0 0.0 copy-start.3
  695.0 1.4 convolution_subtract_fusion
  696.4 0.0 copy-done.3
  (1 shorter events, 0.0 us)
Async XLA Ops:
  7.2 377.2 %all-reduce.3.cloned.1.call-start = ((), (), s32[]{:S(2)}) async-start(), calls=%async_computation | async-start | bytes 2097152 | tf_op jit(solution)/shard_map/psum | solution.py:506
  11.2 1.6 copy-start
  12.8 0.9 copy-start.1
  231.0 383.9 %all-reduce.5.cloned.1.call-start = ((), (), s32[]{:S(2)}) async-start(), calls=%async_computation.1 | async-start | bytes 4194304 | tf_op jit(solution)/shard_map/psum | solution.py:511
  687.7 3.2 copy-start.2
  692.0 3.0 copy-start.4
  695.0 1.4 copy-start.3
Sparse Core Ops, SparseCore 0:
  231.1 153.2 all-reduce.2
  464.3 150.5 all-reduce.4

commit v2 on v1

--- a/solution.py
+++ b/solution.py
@@ -72,22 +72,6 @@
             work[stop:, stop:] -= contract(below, below, 1, 1)
             inverse_ref[stop:, :] -= product(below, solved)
     inverse_ref[...] = jnp.where(at_row >= at_col, inverse_ref[...], 0.0)
-
-
-def inverse_factor(gram_matrix):
-    order = gram_matrix.shape[0]
-    block = min(128, order)
-    return pl.pallas_call(
-        functools.partial(factor_kernel, block),
-        out_shape=jax.ShapeDtypeStruct((order, order), jnp.float32),
-        in_specs=[pl.BlockSpec(memory_space=pltpu.VMEM)],
-        out_specs=pl.BlockSpec(memory_space=pltpu.VMEM),
-        scratch_shapes=[
-            pltpu.VMEM((order, order), jnp.float32),
-            pltpu.VMEM((block, 2 * block), jnp.float32),
-        ],
-        cost_estimate=pl.CostEstimate(flops=2 * order**3, bytes_accessed=8 * order**2, transcendentals=order),
-    )(gram_matrix)
 
 
 class Copies:
@@ -495,6 +479,133 @@
     )(scale, matrix, start_vectors)
 
 
+class Places:
+    def __init__(self):
+        self.r, self.c = lax.axis_index("row"), lax.axis_index("col")
+        self.core, self.x = self.r % 2, self.r // 2
+        self.y, self.z = self.c % 4, self.c // 4
+        self.mate = (2 * self.x + 1 - self.core, self.c)
+        self.ring_x = ((self.r + 6) % 8, self.c), ((self.r + 2) % 8, self.c)
+
+    def peer(self, offset):
+        return self.r, (self.c + offset) % 16
+
+
+def all_sum(copies, at, total, result, land_core, land_x, land_plane):
+    order, width = total.shape
+    half, quarter = order // 2, order // 8
+
+    def rows(first, count, ref=total):
+        return ref.at[pl.ds(pl.multiple_of(first, 8), count), :]
+
+    mine, theirs = rows(at.core * half, half), rows((1 - at.core) * half, half)
+    swap = copies.make(theirs, land_core, copies.reserve(1), at.mate)
+    swap.start()
+    swap.wait_recv()
+    mine[...] += land_core[...]
+
+    def part(t, side, ref=total):
+        size = quarter if side is None else quarter // 2
+        return rows(at.core * half + t * quarter + (0 if side is None else side * size), size, ref)
+
+    scatter = Scatter(copies, copies.reserve(6), at.x, at.ring_x, part, lambda i: land_x.at[i])
+    scatter.start()
+    scatter.relay()
+    scatter.finish()
+
+    def piece(t, ref=total):
+        first = at.core * half + at.x * quarter + 8 * (t // 2)
+        lanes = pl.ds(pl.multiple_of((t % 2) * (width // 2), 128), width // 2)
+        return ref.at[pl.ds(pl.multiple_of(first, 8), 8), lanes]
+
+    slots = copies.reserve(15), copies.reserve(15)
+    sent = []
+    for offset in range(1, 16):
+        to = (at.c + offset) % 16
+        copy = copies.make(piece(to), land_plane.at[offset], slots[0] + offset - 1, at.peer(offset))
+        copy.start()
+        sent.append(copy)
+    own = piece(at.c)
+    value = own[...]
+    for offset, copy in enumerate(sent, 1):
+        copy.wait_recv()
+        value = value + land_plane[offset]
+    own = piece(at.c, result)
+    own[...] = value
+    back = []
+    for offset in range(1, 16):
+        copy = copies.make(own, own, slots[1] + offset - 1, at.peer(offset))
+        copy.start()
+        back.append(copy)
+    for copy in back:
+        copy.wait_recv()
+    gather = Gather(copies, copies.reserve(4), at.x, at.ring_x, lambda t, side: part(t, side, result))
+    gather.start()
+    gather.forward()
+    gather.finish()
+    mine = rows(at.core * half, half, result)
+    give = copies.make(mine, mine, copies.reserve(1), at.mate)
+    give.start()
+    for copy in (swap, *sent, *back):
+        copy.wait_send()
+    give.wait()
+
+
+def greet_all(at):
+    barrier = pltpu.get_barrier_semaphore()
+    others = [at.mate, *at.ring_x] + [at.peer(offset) for offset in range(1, 16)]
+    for who in others:
+        pl.semaphore_signal(barrier, inc=1, device_id=who, device_id_type=MESH)
+    pl.semaphore_wait(barrier, len(others))
+
+
+def sum_scratch(order, width):
+    f32 = jnp.float32
+    return [
+        pltpu.VMEM((order, width), f32),
+        pltpu.VMEM((order, width), f32),
+        pltpu.VMEM((order // 2, width), f32),
+        pltpu.VMEM((6, order // 16, width), f32),
+        pltpu.VMEM((16, 8, width // 2), f32),
+        pltpu.VMEM((order, order), f32),
+        pltpu.VMEM((128, 256), f32),
+        pltpu.SemaphoreType.DMA((64,)),
+        pltpu.SemaphoreType.DMA((64,)),
+    ]
+
+
+def early_kernel(count, slab_ref, inverse_ref, total, result, land_core, land_x, land_plane, work, tile, send, recv):
+    at = Places()
+    greet_all(at)
+    slab = slab_ref[...]
+    total[...] = contract(slab, slab, 0, 0)
+    all_sum(Copies(send, recv), at, total, result, land_core, land_x, land_plane)
+    result[...] = result[...] / count
+    factor_kernel(128, result, inverse_ref, work, tile)
+
+
+def late_kernel(
+    count, slab_ref, image_ref, before_ref, basis_ref, projected_ref, residual_ref,
+    inverse_ref, total, result, land_core, land_x, land_plane, work, tile, send, recv,
+):
+    at = Places()
+    greet_all(at)
+    order = slab_ref.shape[1]
+    slab = contract(slab_ref[...], before_ref[...], 1, 1)
+    image = contract(image_ref[...], before_ref[...], 1, 1)
+    total[:, :order] = contract(slab, slab, 0, 0)
+    total[:, order:] = contract(slab, image, 0, 0)
+    all_sum(Copies(send, recv), at, total, result, land_core, land_x, land_plane)
+    result[...] = result[...] / count
+    factor_kernel(128, result.at[:, :order], inverse_ref, work, tile)
+    inverse = inverse_ref[...]
+    basis = contract(slab, inverse, 1, 1)
+    basis_ref[...] = basis
+    projected = contract(product(inverse, result[:, order:]), inverse, 1, 1)
+    projected_ref[...] = projected
+    residual_ref[...] = contract(image, inverse, 1, 1) - product(basis, projected)
+
+
 def on_device(matrix, start_vectors, interval):
     slab_rows, vectors = start_vectors.shape
     total_rows = slab_rows * lax.axis_size("row") * lax.axis_size("col")
@@ -503,18 +614,29 @@
     scale = jnp.stack([center, 1.0 / half_width])
     early, slab, mapped = filtered_blocks(matrix, start_vectors, scale)
 
-    gram = lax.psum(contract(early, early, 0, 0), ("row", "col")) / total_rows
-    before = inverse_factor(gram)
-    slab = contract(slab, before, 1, 1)
-    mapped = contract(mapped, before, 1, 1)
-    pair = jnp.concatenate([slab, mapped], axis=1)
-    sums = lax.psum(contract(slab, pair, 0, 0), ("row", "col")) / total_rows
-    gram, cross = sums[:, :vectors], sums[:, vectors:]
-    inverse = inverse_factor(gram)
-    basis = contract(slab, inverse, 1, 1)
-    projected = contract(product(inverse, cross), inverse, 1, 1)
-    residual = contract(mapped, inverse, 1, 1) - product(basis, projected)
-    return basis, projected, residual
+    f32 = jnp.float32
+    vmem = pl.BlockSpec(memory_space=pltpu.VMEM)
+    square = jax.ShapeDtypeStruct((vectors, vectors), f32)
+    tall = jax.ShapeDtypeStruct((slab_rows, vectors), f32)
+    cost = pl.CostEstimate(flops=2 * vectors**3, bytes_accessed=8 * vectors**2, transcendentals=vectors)
+    before = pl.pallas_call(
+        functools.partial(early_kernel, total_rows),
+        out_shape=square,
+        in_specs=[vmem],
+        out_specs=vmem,
+        scratch_shapes=sum_scratch(vectors, vectors),
+        compiler_params=pltpu.CompilerParams(collective_id=1, has_side_effects=True, vmem_limit_bytes=40 * 2**20),
+        cost_estimate=cost,
+    )(early)
+    return pl.pallas_call(
+        functools.partial(late_kernel, total_rows),
+        out_shape=(tall, square, tall),
+        in_specs=[vmem] * 3,
+        out_specs=(vmem,) * 3,
+        scratch_shapes=[pltpu.VMEM((vectors, vectors), f32)] + sum_scratch(vectors, 2 * vectors),
+        compiler_params=pltpu.CompilerParams(collective_id=2, has_side_effects=True, vmem_limit_bytes=40 * 2**20),
+        cost_estimate=cost,
+    )(slab, mapped, before)
 
 
 def solution(mesh):

time: 707 us -> 457 us (0.65)
  waiting for transfers between devices: 304 us -> 0 us
  Pallas kernels: 355 us -> 444 us
  matrix products: 18.5 us -> 0 us
  between operations: 17.2 us -> 3.73 us
    psum x2 -> x0, waiting for transfers between devices: 304 us -> none  [the longest x1 153 us: on_device(): gram = lax.psum(contract(early, early, 0, 0), ('row', 'col')) / total_rows]
    pallas_call x2, Pallas kernels: 140 us -> 229 us  [the longest x1 122 us: on_device(): pl.pallas_call(functools.partial(late_kernel, total_rows), out_shape=(tal...]
    dot_general x9 -> x0, matrix products: 18.5 us -> none  [the longest x7 13.9 us: contract(): lax.dot_general(left, right, (((left_dim,), (right_dim,)), ((), ())), pre...]
  transfers between devices with their start and end apart: 2 -> 0, of which waited for: 2 -> 0; matrix products, arithmetic and copies ran while one was open for 0% -> 0% of each run, Pallas kernels for 0% -> 0%
where the time goes in v2:
time: 457 us; the launch traced here: 454 us
  Pallas kernels  444 us (97%)
  local copies, waits for them, and re-layouts  6.09 us (1%)
    pallas_call x1, Pallas kernels, filtered_blocks(): pl.pallas_call(filter_kernel, out_shape=[jax.ShapeDtypeStruct((slab, vect...  215 us
    pallas_call x1, Pallas kernels, on_device(): pl.pallas_call(functools.partial(late_kernel, total_rows), out_shape=(tal...  122 us
    pallas_call x1, Pallas kernels, on_device(): pl.pallas_call(functools.partial(early_kernel, total_rows), out_shape=squ...  107 us

profile of v2, /device:TPU:1, one launch (start us, length us, event | category | flops | bytes accessed | tf_op | source)
XLA Modules:
  0.0 454.0 jit_solution(14402748542293747175)
XLA Ops:
  0.6 1.3 fusion
  4.6 0.1 pad_maximum_fusion.scale_ref
  4.7 0.0 copy-start
  4.7 1.6 copy-done
  6.2 0.0 copy-start.1
  6.2 0.9 copy-done.1
  7.1 215.1 %shard_map.58 = (f32[64,512]{1,0:T(8,128)S(1)}, f32[64,512]{1,0:T(8,128)S(1)}, f32[64,512]{1,0:T(8,128)S(1)}) custom-call(f32[2]{0:T(128)S(1)} %pad_maximum_fusion.scale_ref, f32[1024,512]{1,0:T(8,128)S(1)} %copy-done, f32[64,512]{1,0:T(8,128)S(1)} %copy-done.1), custom_call_target="tpu_custom_call" | custom-call | flops 10000000000 | bytes 4000000 | tf_op jit(solution)/shard_map/pallas_call | solution.py:447
  222.2 107.4 %shard_map.59.before_ref = f32[512,512]{1,0:T(8,128)S(1)} custom-call(f32[64,512]{1,0:T(8,128)S(1)} %get-tuple-element.8.slab_ref), custom_call_target="tpu_custom_call" | custom-call | flops 268435456 | bytes 2097152 | tf_op jit(solution)/shard_map/pallas_call | solution.py:622
  329.6 121.7 %shard_map.60 = (f32[64,512]{1,0:T(8,128)S(1)}, f32[512,512]{1,0:T(8,128)S(1)}, f32[64,512]{1,0:T(8,128)S(1)}) custom-call(f32[64,512]{1,0:T(8,128)S(1)} %get-tuple-element.6.slab_ref, f32[64,512]{1,0:T(8,128)S(1)} %get-tuple-element.7.image_ref, f32[512,512]{1,0:T(8,128)S(1)} %shard_map.59.before_ref), custom_call_target="tpu_custom_call" | custom-call | flops 268435456 | bytes 2097152 | tf_op jit(solution)/shard_map/pallas_call | solution.py:631
  451.3 0.7 copy.9
  451.9 1.0 copy.10
  452.9 0.7 copy.11
Async XLA Ops:
  4.7 1.6 copy-start
  6.2 0.9 copy-start.1

commit v3 on v2

--- a/solution.py
+++ b/solution.py
@@ -28,23 +28,68 @@
     )
 
 
-def factor_panel(panel, first):
-    rows = panel.shape[0]
-    row_at = lax.broadcasted_iota(jnp.int32, panel.shape, 0)
-    pivots = jnp.ones((rows, 1), jnp.float32)
-    pivot_at = lax.broadcasted_iota(jnp.int32, (rows, 1), 0)
-    for step in range(rows):
-        column = panel[:, first + step : first + step + 1]
-        pivot = column[step : step + 1, :]
-        pivots = jnp.where(pivot_at == step, pivot, pivots)
-        if step < rows - 1:
-            multiplier = column / pivot
-            change = multiplier * panel[step : step + 1, :]
-            panel = jnp.where(row_at > step, panel - change, panel)
-    return panel * lax.rsqrt(pivots)
-
-
-def factor_kernel(block, gram_ref, inverse_ref, work, tile):
+def lane_columns(rows, first):
+    narrow = rows[:, :128]
+    lanes = jnp.zeros((PANEL, 128), jnp.int32) + first
+    return [jnp.take_along_axis(narrow, lanes + j, axis=1) for j in range(PANEL)]
+
+
+def row_of(value, step):
+    return jnp.broadcast_to(value[step : step + 1, :], value.shape)
+
+
+def factor_block(tile, pending):
+    block = tile.shape[1] // 2
+    sub = lax.broadcasted_iota(jnp.int32, (PANEL, 128), 0)
+    lane = lax.broadcasted_iota(jnp.int32, (PANEL, block), 1)
+    pending[...] = jnp.zeros_like(pending)
+
+    def panel(p, carry):
+        first = pl.multiple_of(p * PANEL, PANEL)
+        here, after = pl.ds(first, PANEL), pl.ds(pl.multiple_of(first + PANEL, PANEL), PANEL)
+        rows = tile[here, :]
+        late = pending[...]
+        tile[:block, :] -= contract(jnp.where(lane >= first + PANEL, late[:, :block], 0.0), late, 0, 0)
+
+        columns = lane_columns(rows, first)
+        left, right = rows[:, :block], rows[:, block:]
+        inverses = []
+        pivots = jnp.ones((PANEL, 128), jnp.float32)
+        for s in range(PANEL):
+            pivot = row_of(columns[s], s)
+            pivots = jnp.where(sub == s, pivot, pivots)
+            inverse = 1.0 / pivot
+            inverses.append(inverse)
+            if s < PANEL - 1:
+                ratio = jnp.where(sub > s, columns[s] * inverse, 0.0)
+                for j in range(s + 1, PANEL):
+                    columns[j] = columns[j] - ratio * row_of(columns[j], s)
+                left = left - ratio * row_of(left, s)
+                right = right - ratio * row_of(right, s)
+
+        following = tile[after, :]
+        others = lane_columns(following, first)
+        next_left, next_right = following[:, :block], following[:, block:]
+        for s in range(PANEL):
+            ratio = others[s] * inverses[s]
+            for j in range(s + 1, PANEL):
+                others[j] = others[j] - ratio * row_of(columns[j], s)
+            next_left = next_left - ratio * row_of(left, s)
+            next_right = next_right - ratio * row_of(right, s)
+        tile[after, :block] = next_left
+        tile[after, block:] = next_right
+        scale = lax.rsqrt(pivots)
+        left, right = left * scale, right * scale
+        tile[here, :block] = left
+        tile[here, block:] = right
+        pending[:, :block] = left
+        pending[:, block:] = right
+        return carry
+
+    lax.fori_loop(0, block // PANEL, panel, 0)
+
+
+def factor_kernel(block, gram_ref, inverse_ref, work, tile, pending):
     order = gram_ref.shape[0]
     work[...] = gram_ref[...]
     at_row = lax.broadcasted_iota(jnp.int32, (order, order), 0)
@@ -54,24 +99,29 @@
         lax.broadcasted_iota(jnp.int32, (block, block), 0)
         == lax.broadcasted_iota(jnp.int32, (block, block), 1)
     ).astype(jnp.float32)
-    for start in range(0, order, block):
-        stop = start + block
-        tile[:, :block] = work[start:stop, start:stop]
-        tile[:, block:] = unit
-        for first in range(0, block, PANEL):
-            last = first + PANEL
-            done = factor_panel(tile[first:last, :], first)
-            tile[first:last, :] = done
-            if last < block:
-                tile[last:, :] -= contract(done[:, :block], done, 0, 0)[last:, :]
-        small = tile[:, block:]
-        solved = product(small, inverse_ref[start:stop, :])
-        inverse_ref[start:stop, :] = solved
-        if stop < order:
-            below = contract(work[stop:, start:stop], small, 1, 1)
-            work[stop:, stop:] -= contract(below, below, 1, 1)
-            inverse_ref[stop:, :] -= product(below, solved)
-    inverse_ref[...] = jnp.where(at_row >= at_col, inverse_ref[...], 0.0)
+
+    def one(b, carry):
+        start = pl.multiple_of(b * block, block)
+        tile[:block, :block] = work[pl.ds(start, block), pl.ds(start, block)]
+        tile[:block, block:] = unit
+        tile[block:, :] = jnp.zeros((PANEL, 2 * block), jnp.float32)
+        factor_block(tile, pending)
+        for k in range(order // block):
+            @pl.when(b == k)
+            def _():
+                at, stop = k * block, (k + 1) * block
+                row = lax.broadcasted_iota(jnp.int32, (block, block), 0)
+                col = lax.broadcasted_iota(jnp.int32, (block, block), 1)
+                small = jnp.where(row >= col, tile[:block, block:], 0.0)
+                solved = product(small, inverse_ref[at:stop, :stop])
+                inverse_ref[at:stop, :stop] = solved
+                if stop < order:
+                    below = contract(work[stop:, at:stop], small, 1, 1)
+                    work[stop:, stop:] -= contract(below, below, 1, 1)
+                    inverse_ref[stop:, :stop] -= product(below, solved)
+        return carry
+
+    lax.fori_loop(0, order // block, one, 0)
 
 
 class Copies:
@@ -568,25 +618,26 @@
         pltpu.VMEM((6, order // 16, width), f32),
         pltpu.VMEM((16, 8, width // 2), f32),
         pltpu.VMEM((order, order), f32),
-        pltpu.VMEM((128, 256), f32),
+        pltpu.VMEM((128 + PANEL, 256), f32),
+        pltpu.VMEM((PANEL, 256), f32),
         pltpu.SemaphoreType.DMA((64,)),
         pltpu.SemaphoreType.DMA((64,)),
     ]
 
 
-def early_kernel(count, slab_ref, inverse_ref, total, result, land_core, land_x, land_plane, work, tile, send, recv):
+def early_kernel(count, slab_ref, inverse_ref, total, result, land_core, land_x, land_plane, work, tile, pending, send, recv):
     at = Places()
     greet_all(at)
     slab = slab_ref[...]
     total[...] = contract(slab, slab, 0, 0)
     all_sum(Copies(send, recv), at, total, result, land_core, land_x, land_plane)
     result[...] = result[...] / count
-    factor_kernel(128, result, inverse_ref, work, tile)
+    factor_kernel(128, result, inverse_ref, work, tile, pending)
 
 
 def late_kernel(
     count, slab_ref, image_ref, before_ref, basis_ref, projected_ref, residual_ref,
-    inverse_ref, total, result, land_core, land_x, land_plane, work, tile, send, recv,
+    inverse_ref, total, result, land_core, land_x, land_plane, work, tile, pending, send, recv,
 ):
     at = Places()
     greet_all(at)
@@ -597,7 +648,7 @@
     total[:, order:] = contract(slab, image, 0, 0)
     all_sum(Copies(send, recv), at, total, result, land_core, land_x, land_plane)
     result[...] = result[...] / count
-    factor_kernel(128, result.at[:, :order], inverse_ref, work, tile)
+    factor_kernel(128, result.at[:, :order], inverse_ref, work, tile, pending)
     inverse = inverse_ref[...]
     basis = contract(slab, inverse, 1, 1)
     basis_ref[...] = basis

time: 457 us -> 381 us (0.83)
  Pallas kernels: 444 us -> 371 us
    pallas_call x1, Pallas kernels: 107 us -> 70.5 us  [on_device(): pl.pallas_call(functools.partial(early_kernel, total_rows), out_shape=squ...]
    pallas_call x1, Pallas kernels: 122 us -> 85.6 us  [on_device(): pl.pallas_call(functools.partial(late_kernel, total_rows), out_shape=(tal...]
where the time goes in v3:
time: 381 us
  Pallas kernels  371 us (97%)
  local copies, waits for them, and re-layouts  6.09 us (2%)
    pallas_call x1, Pallas kernels, filtered_blocks(): pl.pallas_call(filter_kernel, out_shape=[jax.ShapeDtypeStruct((slab, vect...  215 us
    pallas_call x1, Pallas kernels, on_device(): pl.pallas_call(functools.partial(late_kernel, total_rows), out_shape=(tal...  85.6 us
    pallas_call x1, Pallas kernels, on_device(): pl.pallas_call(functools.partial(early_kernel, total_rows), out_shape=squ...  70.5 us

profile of v3, /device:TPU:1, one launch (start us, length us, event | category | flops | bytes accessed | tf_op | source)
XLA Modules:
  0.0 380.7 jit_solution(18439843807517441136)
XLA Ops:
  0.6 1.3 fusion
  4.6 0.1 pad_maximum_fusion.scale_ref
  4.7 0.0 copy-start
  4.7 1.6 copy-done
  6.2 0.0 copy-start.1
  6.2 0.9 copy-done.1
  7.1 215.2 %shard_map.58 = (f32[64,512]{1,0:T(8,128)S(1)}, f32[64,512]{1,0:T(8,128)S(1)}, f32[64,512]{1,0:T(8,128)S(1)}) custom-call(f32[2]{0:T(128)S(1)} %pad_maximum_fusion.scale_ref, f32[1024,512]{1,0:T(8,128)S(1)} %copy-done, f32[64,512]{1,0:T(8,128)S(1)} %copy-done.1), custom_call_target="tpu_custom_call" | custom-call | flops 10000000000 | bytes 4000000 | tf_op jit(solution)/shard_map/pallas_call | solution.py:497
  222.4 70.5 %shard_map.59.before_ref = f32[512,512]{1,0:T(8,128)S(1)} custom-call(f32[64,512]{1,0:T(8,128)S(1)} %get-tuple-element.8.slab_ref), custom_call_target="tpu_custom_call" | custom-call | flops 268435456 | bytes 2097152 | tf_op jit(solution)/shard_map/pallas_call | solution.py:673
  292.9 85.6 %shard_map.60 = (f32[64,512]{1,0:T(8,128)S(1)}, f32[512,512]{1,0:T(8,128)S(1)}, f32[64,512]{1,0:T(8,128)S(1)}) custom-call(f32[64,512]{1,0:T(8,128)S(1)} %get-tuple-element.6.slab_ref, f32[64,512]{1,0:T(8,128)S(1)} %get-tuple-element.7.image_ref, f32[512,512]{1,0:T(8,128)S(1)} %shard_map.59.before_ref), custom_call_target="tpu_custom_call" | custom-call | flops 268435456 | bytes 2097152 | tf_op jit(solution)/shard_map/pallas_call | solution.py:682
  378.5 0.7 copy.9
  379.1 1.0 copy.10
  380.1 0.7 copy.11
Async XLA Ops:
  4.7 1.6 copy-start
  6.2 0.9 copy-start.1

commit v4 on v3

--- a/solution.py
+++ b/solution.py
@@ -222,11 +222,15 @@
     return one(left[0], right[0]) + (one(left[0], right[1]) + one(left[1], right[0]))
 
 
+STREAMS = 2
+LEAD = 6
+
+
 def filter_kernel(
-    scale_ref, block_ref, start_ref, first_ref, last_ref, image_ref,
-    other, high, low, rows, row_parts, cols, col_parts, vec_high, vec_low,
+    interval_ref, block_ref, start_ref, first_ref, last_ref, image_ref,
+    block, other, high, low, rows, row_parts, cols, col_parts, vec_high, vec_low,
     land_big, land_small, land_col, row_prev, col_prev, first_part,
-    start_land, first_land, last_land, image_land, send, recv,
+    start_land, first_land, last_land, image_land, send, recv, local_sem,
 ):
     r, c = lax.axis_index("row"), lax.axis_index("col")
     core, x, y, z = r % 2, r // 2, c % 4, c // 4
@@ -241,6 +245,8 @@
     ring_z = device(x, core, y, (z + 3) % 4), device(x, core, y, (z + 1) % 4)
     crossed = x != z
 
+    local = pltpu.make_async_copy(block_ref, block, local_sem)
+    local.start()
     barrier = pltpu.get_barrier_semaphore()
 
     def greet(who):
@@ -256,7 +262,7 @@
 
     pl.semaphore_wait(barrier, jnp.where(crossed, 9, 7))
 
-    block_rows, block_cols = block_ref.shape
+    block_rows, block_cols = block.shape
     slab = start_ref.shape[0]
     width = start_ref.shape[1] // 2
     mine_cols = pl.ds(pl.multiple_of(core * width, width), width)
@@ -267,7 +273,10 @@
     block_copy = copies.make(block_ref, other, copies.reserve(1), mate)
     block_copy.start()
 
-    center, inverse_width = scale_ref[0], scale_ref[1]
+    lower_end = jnp.full((1, block_cols), interval_ref[0], jnp.float32)
+    upper_end = jnp.full((1, block_cols), interval_ref[1], jnp.float32)
+    center = 0.5 * (lower_end + upper_end)
+    inverse_width = 1.0 / (0.5 * (upper_end - lower_end))
 
     def prepare(source, which):
         base = which * block_rows
@@ -285,10 +294,7 @@
             high[to, :] = big
             low[to, :] = small
 
-    prepare(block_ref, core)
-
     start_copy.wait_recv()
-    half = width // 2
     own = start_ref[:, mine_cols]
     theirs = start_land[...]
     lower = jnp.where(core == 0, own, theirs)
@@ -296,176 +302,190 @@
     piece = jnp.concatenate([lower, upper], axis=0).T
     cols[x] = piece
     col_prev[...] = piece
-    row_prev[...] = jnp.zeros_like(row_prev)
-    start_copy.wait_send()
-
-    def col_slice(ref):
-        def part(t, side):
-            if side is None:
-                return ref.at[t]
-            return ref.at[t, pl.ds(side * half, half), :]
-        return part
-
-    def plane_slice(ref, colour, axis):
-        def part(t, side):
-            size = half if side is None else half // 2
-            at = pl.ds(colour * half + (0 if side is None else side * size), size)
-            return ref.at[:, t, at, :] if axis == "z" else ref.at[t, :, at, :]
-        return part
-
-    def line_slice(ref, colour, axis):
-        def part(t, side):
-            size = half if side is None else half // 2
-            at = pl.ds(colour * half + (0 if side is None else side * size), size)
-            return ref.at[y, t, at, :] if axis == "z" else ref.at[t, z, at, :]
-        return part
 
     places = {"y": y, "z": z}
     rings = {"y": ring_y, "z": ring_z}
     orders = (("z", "y"), ("y", "z"))
-
-    scatter_slots = [[copies.reserve(6) for _ in range(2)] for _ in range(2)]
-    gather_slots = [[copies.reserve(4) for _ in range(2)] for _ in range(2)]
-    col_slots = copies.reserve(6), copies.reserve(4)
-
-    def scatter_stage(colour, stage):
-        axis = orders[colour][stage]
-        ref_slice = (plane_slice if stage == 0 else line_slice)(row_parts, colour, axis)
-        land = (lambda i: land_big.at[colour, i]) if stage == 0 else (lambda i: land_small.at[colour, i])
-        return Scatter(copies, scatter_slots[colour][stage], places[axis], rings[axis], ref_slice, land)
-
-    def gather_stage(colour, stage):
-        axis = orders[colour][1 - stage]
-        ref_slice = (line_slice if stage == 0 else plane_slice)(rows, colour, axis)
-        return Gather(copies, gather_slots[colour][stage], places[axis], rings[axis], ref_slice)
-
-    col_gather = Gather(copies, col_slots[1], x, ring_x, col_slice(cols))
-    col_scatter = Scatter(copies, col_slots[0], x, ring_x, col_slice(col_parts), lambda i: land_col.at[i])
-
-    col_gather.start()
-    col_gather.forward()
-    col_gather.finish()
-
+    share = width // STREAMS
+    half = share // 2
+
+    class Stream:
+        def __init__(self, index):
+            self.base = index * share
+            self.all = pl.ds(self.base, share)
+            slots = [[copies.reserve(6) for _ in range(2)] for _ in range(2)]
+            self.scatters = [[self.scatter(index, u, stage, slots[u][stage]) for stage in range(2)] for u in range(2)]
+            slots = [[copies.reserve(4) for _ in range(2)] for _ in range(2)]
+            self.gathers = [[self.gather(u, stage, slots[u][stage]) for stage in range(2)] for u in range(2)]
+            self.col_scatter = Scatter(
+                copies, copies.reserve(6), x, ring_x, self.col_slice(col_parts), lambda i: land_col.at[index, i]
+            )
+            self.col_gather = Gather(copies, copies.reserve(4), x, ring_x, self.col_slice(cols))
+
+        def span(self, colour, side):
+            size = half if side is None else half // 2
+            return pl.ds(self.base + colour * half + (0 if side is None else side * size), size)
+
+        def col_slice(self, ref):
+            def part(t, side):
+                return ref.at[t, self.all if side is None else self.span(side, None), :]
+            return part
+
+        def plane(self, ref, colour, axis):
+            def part(t, side):
+                at = self.span(colour, side)
+                return ref.at[:, t, at, :] if axis == "z" else ref.at[t, :, at, :]
+            return part
+
+        def line(self, ref, colour, axis):
+            def part(t, side):
+                at = self.span(colour, side)
+                return ref.at[y, t, at, :] if axis == "z" else ref.at[t, z, at, :]
+            return part
+
+        def scatter(self, index, colour, stage, slot):
+            axis = orders[colour][stage]
+            part = (self.plane if stage == 0 else self.line)(row_parts, colour, axis)
+            landing = land_big if stage == 0 else land_small
+            return Scatter(copies, slot, places[axis], rings[axis], part, lambda i: landing.at[index, colour, i])
+
+        def gather(self, colour, stage, slot):
+            axis = orders[colour][1 - stage]
+            part = (self.line if stage == 0 else self.plane)(rows, colour, axis)
+            return Gather(copies, slot, places[axis], rings[axis], part)
+
+        def multiply(self):
+            for q in range(4):
+                big, small = split(cols[q, self.all, :])
+                vec_high[self.all, q * CHUNK : (q + 1) * CHUNK] = big
+                vec_low[self.all, q * CHUNK : (q + 1) * CHUNK] = small
+
+            @pl.loop(0, 8)
+            def _(i):
+                at = pl.ds(pl.multiple_of(i * 256, 256), 256)
+                left = vec_high[self.all, :], vec_low[self.all, :]
+                out = three_pass(left, (high[at, :], low[at, :]), ((1,), (1,)))
+                row_parts[i // 2, 2 * (i % 2), self.all, :] = out[:, :CHUNK]
+                row_parts[i // 2, 2 * (i % 2) + 1, self.all, :] = out[:, CHUNK:]
+
+        def multiply_turned(self):
+            for q in range(4):
+                col_parts[q, self.all, :] = jnp.zeros((share, CHUNK), jnp.float32)
+
+            @pl.loop(0, 8)
+            def _(i):
+                at = pl.ds(pl.multiple_of(i * 256, 256), 256)
+                pair = [rows[i // 2, 2 * (i % 2) + k, self.all, :] for k in range(2)]
+                out = three_pass(split(jnp.concatenate(pair, axis=1)), (high[at, :], low[at, :]), ((1,), (0,)))
+                for q in range(4):
+                    col_parts[q, self.all, :] += out[:, q * CHUNK : (q + 1) * CHUNK]
+
+        def to_rows(self):
+            self.multiply()
+            firsts = [self.scatters[0][0], self.scatters[1][0]]
+            seconds = [self.scatters[0][1], self.scatters[1][1]]
+            for first in firsts:
+                first.start()
+            yield
+            for first in firsts:
+                first.relay()
+            yield
+            for first, second in zip(firsts, seconds):
+                first.finish()
+                second.start()
+            yield
+            for second in seconds:
+                second.relay()
+            yield
+
+        def run(self):
+            for step in range(3):
+                yield from self.to_rows()
+                for colour in range(2):
+                    self.scatters[colour][1].finish()
+                    at = self.span(colour, None)
+                    value = row_parts[y, z, at, :]
+                    if step > 0:
+                        value = 2.0 * value - row_prev[at, :]
+                    rows[y, z, at, :] = value
+                    row_prev[at, :] = value
+                    if step == 1:
+                        first_part[at, :] = value
+                    self.gathers[colour][0].start()
+                yield
+                for colour in range(2):
+                    self.gathers[colour][0].forward()
+                yield
+                for colour in range(2):
+                    self.gathers[colour][0].finish()
+                    self.gathers[colour][1].start()
+                yield
+                for colour in range(2):
+                    self.gathers[colour][1].forward()
+                yield
+                for colour in range(2):
+                    self.gathers[colour][1].finish()
+                self.multiply_turned()
+                self.col_scatter.start()
+                yield
+                self.col_scatter.relay()
+                yield
+                self.col_scatter.finish()
+                value = col_parts[x, self.all, :]
+                if step != 1:
+                    value = 2.0 * value - col_prev[self.all, :]
+                cols[x, self.all, :] = value
+                col_prev[self.all, :] = value
+                self.col_gather.start()
+                yield
+                self.col_gather.forward()
+                yield
+                self.col_gather.finish()
+            yield from self.to_rows()
+            for colour in range(2):
+                self.scatters[colour][1].finish()
+
+    streams = [Stream(index) for index in range(STREAMS)]
+    for stream in streams:
+        stream.col_gather.start()
+    local.wait()
+    prepare(block, core)
+    for stream in streams:
+        stream.col_gather.forward()
+    start_copy.wait_send()
     block_copy.wait_recv()
     prepare(other, 1 - core)
     block_copy.wait_send()
-
-    def to_rows():
-        for q in range(4):
-            big, small = split(cols[q])
-            vec_high[:, q * CHUNK : (q + 1) * CHUNK] = big
-            vec_low[:, q * CHUNK : (q + 1) * CHUNK] = small
-
-        @pl.loop(0, 8)
-        def _(i):
-            at = pl.ds(pl.multiple_of(i * 256, 256), 256)
-            out = three_pass((vec_high[...], vec_low[...]), (high[at, :], low[at, :]), ((1,), (1,)))
-            row_parts[i // 2, 2 * (i % 2)] = out[:, :CHUNK]
-            row_parts[i // 2, 2 * (i % 2) + 1] = out[:, CHUNK:]
-
-        stages = [scatter_stage(0, 0), scatter_stage(1, 0)]
-        for stage in stages:
-            stage.start()
-        for stage in stages:
-            stage.relay()
-        seconds = [scatter_stage(0, 1), scatter_stage(1, 1)]
-        for stage, second in zip(stages, seconds):
-            stage.finish()
-            second.start()
-        for second in seconds:
-            second.relay()
-        return seconds
-
-    def sweep(step, carry):
-        factor = jnp.where(step == 0, 1.0, 2.0)
-        weight = jnp.where(step == 0, 0.0, 1.0)
-        seconds = to_rows()
-        gathers = []
-        for colour, second in enumerate(seconds):
-            second.finish()
-            at = pl.ds(colour * half, half)
-            value = factor * row_parts[y, z, at, :] - weight * row_prev[at, :]
-            rows[y, z, at, :] = value
-            row_prev[at, :] = value
-            first = gather_stage(colour, 0)
-            first.start()
-            gathers.append(first)
-
-        @pl.when(step == 1)
-        def _():
-            first_part[...] = row_prev[...]
-
-        for first in gathers:
-            first.forward()
-        lasts = []
-        for colour, first in enumerate(gathers):
-            first.finish()
-            last = gather_stage(colour, 1)
-            last.start()
-            lasts.append(last)
-        for last in lasts:
-            last.forward()
-        for last in lasts:
-            last.finish()
-
-        for q in range(4):
-            col_parts[q] = jnp.zeros((width, CHUNK), jnp.float32)
-
-        @pl.loop(0, 8)
-        def _(i):
-            at = pl.ds(pl.multiple_of(i * 256, 256), 256)
-            vec = jnp.concatenate([rows[i // 2, 2 * (i % 2)], rows[i // 2, 2 * (i % 2) + 1]], axis=1)
-            out = three_pass(split(vec), (high[at, :], low[at, :]), ((1,), (0,)))
-            for q in range(4):
-                col_parts[q] += out[:, q * CHUNK : (q + 1) * CHUNK]
-
-        col_scatter.start()
-        col_scatter.relay()
-        col_scatter.finish()
-        again = jnp.where(step == 1, 1.0, 2.0)
-        minus = jnp.where(step == 1, 0.0, 1.0)
-        value = again * col_parts[x] - minus * col_prev[...]
-        cols[x] = value
-        col_prev[...] = value
-        col_gather.start()
-        col_gather.forward()
-        col_gather.finish()
-        return carry
-
-    lax.fori_loop(0, 3, sweep, 0)
-    for second in to_rows():
-        second.finish()
-
-    def trade(piece, land, out_ref):
-        turned = piece.T
-        land[1] = turned
-        copy = copies.make(
-            land.at[1, pl.ds(pl.multiple_of((1 - core) * slab, slab), slab), :],
-            land.at[0, pl.ds(pl.multiple_of((1 - core) * slab, slab), slab), :],
-            copies.reserve(1),
-            mate,
-        )
+    for stream in streams:
+        stream.col_gather.finish()
+
+    runs = [stream.run() for stream in streams]
+    for _ in range(LEAD):
+        next(runs[0])
+    going = True
+    while going:
+        going = False
+        for run in runs:
+            if next(run, "end") != "end":
+                going = True
+
+    def trade(piece, land):
+        land[1] = piece.T
+        rows_there = pl.ds(pl.multiple_of((1 - core) * slab, slab), slab)
+        copy = copies.make(land.at[1, rows_there, :], land.at[0, rows_there, :], copies.reserve(1), mate)
         copy.start()
         return copy
 
-    first_copy = trade(first_part[...], first_land, first_ref)
-    last_copy = trade(col_prev[...], last_land, last_ref)
+    first_copy = trade(first_part[...], first_land)
+    last_copy = trade(col_prev[...], last_land)
 
     image_land[2, :, :] = row_parts[y, z].T
     image_slots = copies.reserve(2)
-
-    same = copies.make(
-        image_land.at[2, pl.ds(pl.multiple_of(core * slab, slab), slab), :],
-        image_land.at[0, pl.ds(0, slab), :],
-        image_slots,
-        device(z, core, y, x),
-    )
-    cross = copies.make(
-        image_land.at[2, pl.ds(pl.multiple_of((1 - core) * slab, slab), slab), :],
-        image_land.at[1, pl.ds(0, slab), :],
-        image_slots + 1,
-        device(z, 1 - core, y, x),
-    )
+    keep = pl.ds(pl.multiple_of(core * slab, slab), slab)
+    give = pl.ds(pl.multiple_of((1 - core) * slab, slab), slab)
+    top = pl.ds(0, slab)
+    same = copies.make(image_land.at[2, keep, :], image_land.at[0, top, :], image_slots, device(z, core, y, x))
+    cross = copies.make(image_land.at[2, give, :], image_land.at[1, top, :], image_slots + 1, device(z, 1 - core, y, x))
     cross.start()
 
     @pl.when(crossed)
@@ -475,31 +495,31 @@
 
     @pl.when(jnp.logical_not(crossed))
     def _():
-        image_land[0, pl.ds(0, slab), :] = image_land[2, pl.ds(pl.multiple_of(core * slab, slab), slab), :]
-
-    keep = pl.ds(pl.multiple_of(core * slab, slab), slab)
+        image_land[0, top, :] = image_land[2, keep, :]
+
     for copy, land, out_ref in ((first_copy, first_land, first_ref), (last_copy, last_land, last_ref)):
         copy.wait()
         out_ref[:, mine_cols] = land[1, keep, :]
         out_ref[:, mate_cols] = land[0, keep, :]
     cross.wait()
-    image_ref[:, mine_cols] = image_land[0, pl.ds(0, slab), :]
-    image_ref[:, mate_cols] = image_land[1, pl.ds(0, slab), :]
-
-
-def filtered_blocks(matrix, start_vectors, scale):
+    image_ref[:, mine_cols] = image_land[0, top, :]
+    image_ref[:, mate_cols] = image_land[1, top, :]
+
+
+def filtered_blocks(matrix, start_vectors, interval):
     block_rows, block_cols = matrix.shape
     slab, vectors = start_vectors.shape
     width = vectors // 2
-    half = width // 2
+    share = width // STREAMS
     f32, bf16 = jnp.float32, jnp.bfloat16
     vmem = pl.BlockSpec(memory_space=pltpu.VMEM)
     return pl.pallas_call(
         filter_kernel,
         out_shape=[jax.ShapeDtypeStruct((slab, vectors), f32)] * 3,
-        in_specs=[pl.BlockSpec(memory_space=pltpu.SMEM), vmem, vmem],
+        in_specs=[pl.BlockSpec(memory_space=pltpu.SMEM), pl.BlockSpec(memory_space=pl.ANY), vmem],
         out_specs=[vmem] * 3,
         scratch_shapes=[
+            pltpu.VMEM((block_rows, block_cols), f32),
             pltpu.VMEM((block_rows, block_cols), f32),
             pltpu.VMEM((2 * block_rows, block_cols), bf16),
             pltpu.VMEM((2 * block_rows, block_cols), bf16),
@@ -509,9 +529,9 @@
             pltpu.VMEM((4, width, CHUNK), f32),
             pltpu.VMEM((width, block_cols), bf16),
             pltpu.VMEM((width, block_cols), bf16),
-            pltpu.VMEM((2, 6, 4, half // 2, CHUNK), f32),
-            pltpu.VMEM((2, 6, half // 2, CHUNK), f32),
-            pltpu.VMEM((6, half, CHUNK), f32),
+            pltpu.VMEM((STREAMS, 2, 6, 4, share // 4, CHUNK), f32),
+            pltpu.VMEM((STREAMS, 2, 6, share // 4, CHUNK), f32),
+            pltpu.VMEM((STREAMS, 6, share // 2, CHUNK), f32),
             pltpu.VMEM((width, CHUNK), f32),
             pltpu.VMEM((width, CHUNK), f32),
             pltpu.VMEM((width, CHUNK), f32),
@@ -519,14 +539,15 @@
             pltpu.VMEM((2, CHUNK, width), f32),
             pltpu.VMEM((2, CHUNK, width), f32),
             pltpu.VMEM((3, CHUNK, width), f32),
-            pltpu.SemaphoreType.DMA((64,)),
-            pltpu.SemaphoreType.DMA((64,)),
+            pltpu.SemaphoreType.DMA((112,)),
+            pltpu.SemaphoreType.DMA((112,)),
+            pltpu.SemaphoreType.DMA,
         ],
         compiler_params=pltpu.CompilerParams(
-            collective_id=0, has_side_effects=True, vmem_limit_bytes=40 * 2**20
+            collective_id=0, has_side_effects=True, vmem_limit_bytes=50 * 2**20
         ),
         cost_estimate=pl.CostEstimate(flops=10**10, bytes_accessed=4 * 10**6, transcendentals=0),
-    )(scale, matrix, start_vectors)
+    )(interval, matrix, start_vectors)
 
 
 class Places:
@@ -660,10 +681,7 @@
 def on_device(matrix, start_vectors, interval):
     slab_rows, vectors = start_vectors.shape
     total_rows = slab_rows * lax.axis_size("row") * lax.axis_size("col")
-    center = 0.5 * (interval[0] + interval[1])
-    half_width = 0.5 * (interval[1] - interval[0])
-    scale = jnp.stack([center, 1.0 / half_width])
-    early, slab, mapped = filtered_blocks(matrix, start_vectors, scale)
+    early, slab, mapped = filtered_blocks(matrix, start_vectors, interval)
 
     f32 = jnp.float32
     vmem = pl.BlockSpec(memory_space=pltpu.VMEM)

time: 381 us -> 395 us (1.037)
  Pallas kernels: 371 us -> 389 us
    pallas_call x1, Pallas kernels: 215 us -> 234 us  [filtered_blocks(): pl.pallas_call(filter_kernel, out_shape=[jax.ShapeDtypeStruct((slab, vect...]
where the time goes in v4:
time: 395 us
  Pallas kernels  389 us (98%)
  local copies, waits for them, and re-layouts  5.42 us (1%)
    pallas_call x1, Pallas kernels, filtered_blocks(): pl.pallas_call(filter_kernel, out_shape=[jax.ShapeDtypeStruct((slab, vect...  234 us
    pallas_call x1, Pallas kernels, on_device(): pl.pallas_call(functools.partial(late_kernel, total_rows), out_shape=(tal...  85.2 us
    pallas_call x1, Pallas kernels, on_device(): pl.pallas_call(functools.partial(early_kernel, total_rows), out_shape=squ...  69.5 us

profile of v4, /device:TPU:1, one launch (start us, length us, event | category | flops | bytes accessed | tf_op | source)
XLA Modules:
  0.0 394.6 jit_solution(14173652658988576042)
XLA Ops:
  0.6 0.0 copy-start
  0.6 1.6 copy-done
  2.2 0.0 copy-start.1
  2.2 0.9 copy-done.1
  3.1 0.0 copy-start.2
  3.1 0.7 copy-done.2
  3.8 233.8 %shard_map.58 = (f32[64,512]{1,0:T(8,128)S(1)}, f32[64,512]{1,0:T(8,128)S(1)}, f32[64,512]{1,0:T(8,128)S(1)}) custom-call(f32[2]{0:T(128)S(1)} %copy-done.2, f32[1024,512]{1,0:T(8,128)S(1)} %copy-done, f32[64,512]{1,0:T(8,128)S(1)} %copy-done.1), custom_call_target="tpu_custom_call" | custom-call | flops 10000000000 | bytes 4000000 | tf_op jit(solution)/shard_map/pallas_call | solution.py:516
  237.6 69.5 %shard_map.59.before_ref = f32[512,512]{1,0:T(8,128)S(1)} custom-call(f32[64,512]{1,0:T(8,128)S(1)} %get-tuple-element.8.slab_ref), custom_call_target="tpu_custom_call" | custom-call | flops 268435456 | bytes 2097152 | tf_op jit(solution)/shard_map/pallas_call | solution.py:691
  307.1 85.2 %shard_map.60 = (f32[64,512]{1,0:T(8,128)S(1)}, f32[512,512]{1,0:T(8,128)S(1)}, f32[64,512]{1,0:T(8,128)S(1)}) custom-call(f32[64,512]{1,0:T(8,128)S(1)} %get-tuple-element.6.slab_ref, f32[64,512]{1,0:T(8,128)S(1)} %get-tuple-element.7.image_ref, f32[512,512]{1,0:T(8,128)S(1)} %shard_map.59.before_ref), custom_call_target="tpu_custom_call" | custom-call | flops 268435456 | bytes 2097152 | tf_op jit(solution)/shard_map/pallas_call | solution.py:700
  392.3 0.7 copy.9
  393.0 1.0 copy.10
  393.9 0.7 copy.11
Async XLA Ops:
  0.6 1.6 copy-start
  2.2 0.9 copy-start.1
  3.1 0.7 copy-start.2

commit v5 on v4

--- a/solution.py
+++ b/solution.py
@@ -10,6 +10,7 @@
 FILTER_DEG = 3
 OUTER = 2
 PANEL = 8
+BLOCK = 128
 MESH = pl.DeviceIdType.MESH
 CHUNK = 128
 
@@ -38,11 +39,10 @@
     return jnp.broadcast_to(value[step : step + 1, :], value.shape)
 
 
-def factor_block(tile, pending):
+def factor_panels(tile, pending, begin, end):
     block = tile.shape[1] // 2
     sub = lax.broadcasted_iota(jnp.int32, (PANEL, 128), 0)
     lane = lax.broadcasted_iota(jnp.int32, (PANEL, block), 1)
-    pending[...] = jnp.zeros_like(pending)
 
     def panel(p, carry):
         first = pl.multiple_of(p * PANEL, PANEL)
@@ -86,42 +86,34 @@
         pending[:, block:] = right
         return carry
 
-    lax.fori_loop(0, block // PANEL, panel, 0)
-
-
-def factor_kernel(block, gram_ref, inverse_ref, work, tile, pending):
-    order = gram_ref.shape[0]
-    work[...] = gram_ref[...]
+    lax.fori_loop(begin, end, panel, 0)
+
+
+def factor_steps(pieces, work, inverse_ref, tile, pending):
+    order, block = work.shape[0], BLOCK
     at_row = lax.broadcasted_iota(jnp.int32, (order, order), 0)
     at_col = lax.broadcasted_iota(jnp.int32, (order, order), 1)
     inverse_ref[...] = (at_row == at_col).astype(jnp.float32)
-    unit = (
-        lax.broadcasted_iota(jnp.int32, (block, block), 0)
-        == lax.broadcasted_iota(jnp.int32, (block, block), 1)
-    ).astype(jnp.float32)
-
-    def one(b, carry):
-        start = pl.multiple_of(b * block, block)
-        tile[:block, :block] = work[pl.ds(start, block), pl.ds(start, block)]
-        tile[:block, block:] = unit
+    row = lax.broadcasted_iota(jnp.int32, (block, block), 0)
+    col = lax.broadcasted_iota(jnp.int32, (block, block), 1)
+    panels = block // PANEL
+    for at in range(0, order, block):
+        stop = at + block
+        tile[:block, :block] = work[at:stop, at:stop]
+        tile[:block, block:] = (row == col).astype(jnp.float32)
         tile[block:, :] = jnp.zeros((PANEL, 2 * block), jnp.float32)
-        factor_block(tile, pending)
-        for k in range(order // block):
-            @pl.when(b == k)
-            def _():
-                at, stop = k * block, (k + 1) * block
-                row = lax.broadcasted_iota(jnp.int32, (block, block), 0)
-                col = lax.broadcasted_iota(jnp.int32, (block, block), 1)
-                small = jnp.where(row >= col, tile[:block, block:], 0.0)
-                solved = product(small, inverse_ref[at:stop, :stop])
-                inverse_ref[at:stop, :stop] = solved
-                if stop < order:
-                    below = contract(work[stop:, at:stop], small, 1, 1)
-                    work[stop:, stop:] -= contract(below, below, 1, 1)
-                    inverse_ref[stop:, :stop] -= product(below, solved)
-        return carry
-
-    lax.fori_loop(0, order // block, one, 0)
+        pending[...] = jnp.zeros_like(pending)
+        for piece in range(pieces):
+            factor_panels(tile, pending, piece * panels // pieces, (piece + 1) * panels // pieces)
+            yield
+        small = jnp.where(row >= col, tile[:block, block:], 0.0)
+        solved = product(small, inverse_ref[at:stop, :stop])
+        inverse_ref[at:stop, :stop] = solved
+        if stop < order:
+            below = contract(work[stop:, at:stop], small, 1, 1)
+            work[stop:, stop:] -= contract(below, below, 1, 1)
+            inverse_ref[stop:, :stop] -= product(below, solved)
+            yield
 
 
 class Copies:
@@ -222,16 +214,87 @@
     return one(left[0], right[0]) + (one(left[0], right[1]) + one(left[1], right[0]))
 
 
+class TotalSum:
+    def __init__(self, copies, position, mate, ring_x, peers, buffers):
+        core, x, c = position
+        self.total, self.result, self.land_core, land_x, self.land_plane = buffers
+        order, width = self.total.shape
+        half, quarter = order // 2, order // 8
+
+        def rows(ref, first, count):
+            return ref.at[pl.ds(pl.multiple_of(first, 8), count), :]
+
+        def part(ref):
+            def one(t, side):
+                size = quarter if side is None else quarter // 2
+                return rows(ref, core * half + t * quarter + (0 if side is None else side * size), size)
+            return one
+
+        def piece(ref, t):
+            first = core * half + x * quarter + 8 * (t // 2)
+            lanes = pl.ds(pl.multiple_of((t % 2) * (width // 2), 128), width // 2)
+            return ref.at[pl.ds(pl.multiple_of(first, 8), 8), lanes]
+
+        self.mine = rows(self.total, core * half, half)
+        self.swap = copies.make(rows(self.total, (1 - core) * half, half), self.land_core, copies.reserve(1), mate)
+        self.scatter = Scatter(copies, copies.reserve(6), x, ring_x, part(self.total), lambda i: land_x.at[i])
+        self.own, self.summed = piece(self.total, c), piece(self.result, c)
+        self.there, self.back = [], []
+        for offset, peer in peers:
+            source, target = piece(self.total, (c + offset) % 16), self.land_plane.at[offset]
+            self.there.append(copies.make(source, target, copies.reserve(1), peer))
+            self.back.append(copies.make(self.summed, self.summed, copies.reserve(1), peer))
+        self.gather = Gather(copies, copies.reserve(4), x, ring_x, part(self.result))
+        whole = rows(self.result, core * half, half)
+        self.give = copies.make(whole, whole, copies.reserve(1), mate)
+
+    def steps(self):
+        self.swap.start()
+        yield
+        self.swap.wait_recv()
+        self.mine[...] += self.land_core[...]
+        self.scatter.start()
+        yield
+        self.scatter.relay()
+        yield
+        self.scatter.finish()
+        for copy in self.there:
+            copy.start()
+        yield
+        value = self.own[...]
+        for offset, copy in enumerate(self.there, 1):
+            copy.wait_recv()
+            value = value + self.land_plane[offset]
+        self.summed[...] = value
+        for copy in self.back:
+            copy.start()
+        yield
+        for copy in self.back:
+            copy.wait_recv()
+        self.gather.start()
+        yield
+        self.gather.forward()
+        yield
+        self.gather.finish()
+        self.give.start()
+        for copy in (self.swap, *self.there, *self.back):
+            copy.wait_send()
+        yield
+        self.give.wait()
+
+
 STREAMS = 2
-LEAD = 6
-
-
-def filter_kernel(
-    interval_ref, block_ref, start_ref, first_ref, last_ref, image_ref,
+
+
+def whole_kernel(
+    count, interval_ref, block_ref, start_ref, basis_ref, projected_ref, residual_ref,
     block, other, high, low, rows, row_parts, cols, col_parts, vec_high, vec_low,
     land_big, land_small, land_col, row_prev, col_prev, first_part,
-    start_land, first_land, last_land, image_land, send, recv, local_sem,
+    start_land, first_land, last_land, image_land, slab_ref, image_ref, before_ref, inverse_ref,
+    *rest,
 ):
+    sum_buffers = [rest[5 * k : 5 * k + 5] for k in range(3)]
+    tile, pending, send, recv, local_sem = rest[15:]
     r, c = lax.axis_index("row"), lax.axis_index("col")
     core, x, y, z = r % 2, r // 2, c % 4, c // 4
     copies = Copies(send, recv)
@@ -252,7 +315,8 @@
     def greet(who):
         pl.semaphore_signal(barrier, inc=1, device_id=who, device_id_type=MESH)
 
-    for who in (mate, *ring_x, *ring_y, *ring_z):
+    peers = [(offset, (r, (c + offset) % 16)) for offset in range(1, 16)]
+    for who in (mate, *ring_x, *(peer for _, peer in peers)):
         greet(who)
 
     @pl.when(crossed)
@@ -260,7 +324,7 @@
         greet(device(z, core, y, x))
         greet(device(z, 1 - core, y, x))
 
-    pl.semaphore_wait(barrier, jnp.where(crossed, 9, 7))
+    pl.semaphore_wait(barrier, jnp.where(crossed, 20, 18))
 
     block_rows, block_cols = block.shape
     slab = start_ref.shape[0]
@@ -312,6 +376,7 @@
     class Stream:
         def __init__(self, index):
             self.base = index * share
+            self.at_first = self.at_last = False
             self.all = pl.ds(self.base, share)
             slots = [[copies.reserve(6) for _ in range(2)] for _ in range(2)]
             self.scatters = [[self.scatter(index, u, stage, slots[u][stage]) for stage in range(2)] for u in range(2)]
@@ -412,6 +477,7 @@
                     if step == 1:
                         first_part[at, :] = value
                     self.gathers[colour][0].start()
+                self.at_first = step >= 1
                 yield
                 for colour in range(2):
                     self.gathers[colour][0].forward()
@@ -437,6 +503,7 @@
                 cols[x, self.all, :] = value
                 col_prev[self.all, :] = value
                 self.col_gather.start()
+                self.at_last = step == 2
                 yield
                 self.col_gather.forward()
                 yield
@@ -459,65 +526,118 @@
     for stream in streams:
         stream.col_gather.finish()
 
+    keep = pl.ds(pl.multiple_of(core * slab, slab), slab)
+    give = pl.ds(pl.multiple_of((1 - core) * slab, slab), slab)
+    top = pl.ds(0, slab)
+    sums = [TotalSum(copies, (core, x, c), mate, ring_x, peers, buffers) for buffers in sum_buffers]
+
+    def trade(piece, land, target):
+        land[1] = piece.T
+        copy = copies.make(land.at[1, give, :], land.at[0, give, :], copies.reserve(1), mate)
+        copy.start()
+        yield
+        copy.wait()
+        target[:, mine_cols] = land[1, keep, :]
+        target[:, mate_cols] = land[0, keep, :]
+
+    def first_chain():
+        yield from trade(first_part[...], first_land, slab_ref)
+        sums[0].total[...] = contract(slab_ref[...], slab_ref[...], 0, 0)
+        yield from sums[0].steps()
+        sums[0].total[...] = sums[0].result[...] / count
+        yield from factor_steps(2, sums[0].total, before_ref, tile, pending)
+
+    def last_chain():
+        yield from trade(col_prev[...], last_land, slab_ref)
+        slab_ref[...] = contract(slab_ref[...], before_ref[...], 1, 1)
+        sums[1].total[...] = contract(slab_ref[...], slab_ref[...], 0, 0)
+        yield from sums[1].steps()
+        sums[1].total[...] = sums[1].result[...] / count
+        yield from factor_steps(2, sums[1].total, inverse_ref, tile, pending)
+
+    def image_chain():
+        image_land[2, :, :] = row_parts[y, z].T
+        slots = copies.reserve(2)
+        same = copies.make(image_land.at[2, keep, :], image_land.at[0, top, :], slots, device(z, core, y, x))
+        cross = copies.make(image_land.at[2, give, :], image_land.at[1, top, :], slots + 1, device(z, 1 - core, y, x))
+        cross.start()
+
+        @pl.when(crossed)
+        def _():
+            same.start()
+
+        yield
+
+        @pl.when(crossed)
+        def _():
+            same.wait()
+
+        @pl.when(jnp.logical_not(crossed))
+        def _():
+            image_land[0, top, :] = image_land[2, keep, :]
+
+        cross.wait()
+        image_ref[:, mine_cols] = image_land[0, top, :]
+        image_ref[:, mate_cols] = image_land[1, top, :]
+        image_ref[...] = contract(image_ref[...], before_ref[...], 1, 1)
+        sums[2].total[...] = contract(slab_ref[...], image_ref[...], 0, 0)
+        yield from sums[2].steps()
+
+    def advance(chain):
+        return next(chain, "end") != "end"
+
     runs = [stream.run() for stream in streams]
-    for _ in range(LEAD):
-        next(runs[0])
+    chains, begun = [], 0
     going = True
     while going:
         going = False
         for run in runs:
-            if next(run, "end") != "end":
-                going = True
-
-    def trade(piece, land):
-        land[1] = piece.T
-        rows_there = pl.ds(pl.multiple_of((1 - core) * slab, slab), slab)
-        copy = copies.make(land.at[1, rows_there, :], land.at[0, rows_there, :], copies.reserve(1), mate)
-        copy.start()
-        return copy
-
-    first_copy = trade(first_part[...], first_land)
-    last_copy = trade(col_prev[...], last_land)
-
-    image_land[2, :, :] = row_parts[y, z].T
-    image_slots = copies.reserve(2)
-    keep = pl.ds(pl.multiple_of(core * slab, slab), slab)
-    give = pl.ds(pl.multiple_of((1 - core) * slab, slab), slab)
-    top = pl.ds(0, slab)
-    same = copies.make(image_land.at[2, keep, :], image_land.at[0, top, :], image_slots, device(z, core, y, x))
-    cross = copies.make(image_land.at[2, give, :], image_land.at[1, top, :], image_slots + 1, device(z, 1 - core, y, x))
-    cross.start()
-
-    @pl.when(crossed)
-    def _():
-        same.start()
-        same.wait()
-
-    @pl.when(jnp.logical_not(crossed))
-    def _():
-        image_land[0, top, :] = image_land[2, keep, :]
-
-    for copy, land, out_ref in ((first_copy, first_land, first_ref), (last_copy, last_land, last_ref)):
-        copy.wait()
-        out_ref[:, mine_cols] = land[1, keep, :]
-        out_ref[:, mate_cols] = land[0, keep, :]
-    cross.wait()
-    image_ref[:, mine_cols] = image_land[0, top, :]
-    image_ref[:, mate_cols] = image_land[1, top, :]
-
-
-def filtered_blocks(matrix, start_vectors, interval):
+            going = advance(run) or going
+            if chains and not advance(chains[0]):
+                chains.pop(0)
+        if begun == 0 and all(stream.at_first for stream in streams):
+            chains.append(first_chain())
+            begun = 1
+        if begun == 1 and all(stream.at_last for stream in streams):
+            chains.append(last_chain())
+            begun = 2
+    while len(chains) > 1:
+        if not advance(chains[0]):
+            chains.pop(0)
+    chains.append(image_chain())
+    while chains:
+        chains = [chain for chain in reversed(chains) if advance(chain)][::-1]
+
+    inverse = inverse_ref[...]
+    basis = contract(slab_ref[...], inverse, 1, 1)
+    basis_ref[...] = basis
+    projected = contract(product(inverse, sums[2].result[...] / count), inverse, 1, 1)
+    projected_ref[...] = projected
+    residual_ref[...] = contract(image_ref[...], inverse, 1, 1) - product(basis, projected)
+
+
+def on_device(matrix, start_vectors, interval):
     block_rows, block_cols = matrix.shape
     slab, vectors = start_vectors.shape
+    total_rows = slab * lax.axis_size("row") * lax.axis_size("col")
     width = vectors // 2
     share = width // STREAMS
     f32, bf16 = jnp.float32, jnp.bfloat16
     vmem = pl.BlockSpec(memory_space=pltpu.VMEM)
+    tall = jax.ShapeDtypeStruct((slab, vectors), f32)
+    square = jax.ShapeDtypeStruct((vectors, vectors), f32)
+    one_sum = [
+        pltpu.VMEM((vectors, vectors), f32),
+        pltpu.VMEM((vectors, vectors), f32),
+        pltpu.VMEM((vectors // 2, vectors), f32),
+        pltpu.VMEM((6, vectors // 16, vectors), f32),
+        pltpu.VMEM((16, 8, vectors // 2), f32),
+    ]
     return pl.pallas_call(
-        filter_kernel,
-        out_shape=[jax.ShapeDtypeStruct((slab, vectors), f32)] * 3,
+        functools.partial(whole_kernel, total_rows),
+        out_shape=(tall, square, tall),
         in_specs=[pl.BlockSpec(memory_space=pltpu.SMEM), pl.BlockSpec(memory_space=pl.ANY), vmem],
-        out_specs=[vmem] * 3,
+        out_specs=(vmem,) * 3,
         scratch_shapes=[
             pltpu.VMEM((block_rows, block_cols), f32),
             pltpu.VMEM((block_rows, block_cols), f32),
@@ -539,173 +659,22 @@
             pltpu.VMEM((2, CHUNK, width), f32),
             pltpu.VMEM((2, CHUNK, width), f32),
             pltpu.VMEM((3, CHUNK, width), f32),
-            pltpu.SemaphoreType.DMA((112,)),
-            pltpu.SemaphoreType.DMA((112,)),
+            pltpu.VMEM((slab, vectors), f32),
+            pltpu.VMEM((slab, vectors), f32),
+            pltpu.VMEM((vectors, vectors), f32),
+            pltpu.VMEM((vectors, vectors), f32),
+            *(one_sum * 3),
+            pltpu.VMEM((BLOCK + PANEL, 2 * BLOCK), f32),
+            pltpu.VMEM((PANEL, 2 * BLOCK), f32),
+            pltpu.SemaphoreType.DMA((256,)),
+            pltpu.SemaphoreType.DMA((256,)),
             pltpu.SemaphoreType.DMA,
         ],
         compiler_params=pltpu.CompilerParams(
-            collective_id=0, has_side_effects=True, vmem_limit_bytes=50 * 2**20
+            collective_id=0, has_side_effects=True, vmem_limit_bytes=56 * 2**20
         ),
         cost_estimate=pl.CostEstimate(flops=10**10, bytes_accessed=4 * 10**6, transcendentals=0),
     )(interval, matrix, start_vectors)
-
-
-class Places:
-    def __init__(self):
-        self.r, self.c = lax.axis_index("row"), lax.axis_index("col")
-        self.core, self.x = self.r % 2, self.r // 2
-        self.y, self.z = self.c % 4, self.c // 4
-        self.mate = (2 * self.x + 1 - self.core, self.c)
-        self.ring_x = ((self.r + 6) % 8, self.c), ((self.r + 2) % 8, self.c)
-
-    def peer(self, offset):
-        return self.r, (self.c + offset) % 16
-
-
-def all_sum(copies, at, total, result, land_core, land_x, land_plane):
-    order, width = total.shape
-    half, quarter = order // 2, order // 8
-
-    def rows(first, count, ref=total):
-        return ref.at[pl.ds(pl.multiple_of(first, 8), count), :]
-
-    mine, theirs = rows(at.core * half, half), rows((1 - at.core) * half, half)
-    swap = copies.make(theirs, land_core, copies.reserve(1), at.mate)
-    swap.start()
-    swap.wait_recv()
-    mine[...] += land_core[...]
-
-    def part(t, side, ref=total):
-        size = quarter if side is None else quarter // 2
-        return rows(at.core * half + t * quarter + (0 if side is None else side * size), size, ref)
-
-    scatter = Scatter(copies, copies.reserve(6), at.x, at.ring_x, part, lambda i: land_x.at[i])
-    scatter.start()
-    scatter.relay()
-    scatter.finish()
-
-    def piece(t, ref=total):
-        first = at.core * half + at.x * quarter + 8 * (t // 2)
-        lanes = pl.ds(pl.multiple_of((t % 2) * (width // 2), 128), width // 2)
-        return ref.at[pl.ds(pl.multiple_of(first, 8), 8), lanes]
-
-    slots = copies.reserve(15), copies.reserve(15)
-    sent = []
-    for offset in range(1, 16):
-        to = (at.c + offset) % 16
-        copy = copies.make(piece(to), land_plane.at[offset], slots[0] + offset - 1, at.peer(offset))
-        copy.start()
-        sent.append(copy)
-    own = piece(at.c)
-    value = own[...]
-    for offset, copy in enumerate(sent, 1):
-        copy.wait_recv()
-        value = value + land_plane[offset]
-    own = piece(at.c, result)
-    own[...] = value
-    back = []
-    for offset in range(1, 16):
-        copy = copies.make(own, own, slots[1] + offset - 1, at.peer(offset))
-        copy.start()
-        back.append(copy)
-    for copy in back:
-        copy.wait_recv()
-    gather = Gather(copies, copies.reserve(4), at.x, at.ring_x, lambda t, side: part(t, side, result))
-    gather.start()
-    gather.forward()
-    gather.finish()
-    mine = rows(at.core * half, half, result)
-    give = copies.make(mine, mine, copies.reserve(1), at.mate)
-    give.start()
-    for copy in (swap, *sent, *back):
-        copy.wait_send()
-    give.wait()
-
-
-def greet_all(at):
-    barrier = pltpu.get_barrier_semaphore()
-    others = [at.mate, *at.ring_x] + [at.peer(offset) for offset in range(1, 16)]
-    for who in others:
-        pl.semaphore_signal(barrier, inc=1, device_id=who, device_id_type=MESH)
-    pl.semaphore_wait(barrier, len(others))
-
-
-def sum_scratch(order, width):
-    f32 = jnp.float32
-    return [
-        pltpu.VMEM((order, width), f32),
-        pltpu.VMEM((order, width), f32),
-        pltpu.VMEM((order // 2, width), f32),
-        pltpu.VMEM((6, order // 16, width), f32),
-        pltpu.VMEM((16, 8, width // 2), f32),
-        pltpu.VMEM((order, order), f32),
-        pltpu.VMEM((128 + PANEL, 256), f32),
-        pltpu.VMEM((PANEL, 256), f32),
-        pltpu.SemaphoreType.DMA((64,)),
-        pltpu.SemaphoreType.DMA((64,)),
-    ]
-
-
-def early_kernel(count, slab_ref, inverse_ref, total, result, land_core, land_x, land_plane, work, tile, pending, send, recv):
-    at = Places()
-    greet_all(at)
-    slab = slab_ref[...]
-    total[...] = contract(slab, slab, 0, 0)
-    all_sum(Copies(send, recv), at, total, result, land_core, land_x, land_plane)
-    result[...] = result[...] / count
-    factor_kernel(128, result, inverse_ref, work, tile, pending)
-
-
-def late_kernel(
-    count, slab_ref, image_ref, before_ref, basis_ref, projected_ref, residual_ref,
-    inverse_ref, total, result, land_core, land_x, land_plane, work, tile, pending, send, recv,
-):
-    at = Places()
-    greet_all(at)
-    order = slab_ref.shape[1]
-    slab = contract(slab_ref[...], before_ref[...], 1, 1)
-    image = contract(image_ref[...], before_ref[...], 1, 1)
-    total[:, :order] = contract(slab, slab, 0, 0)
-    total[:, order:] = contract(slab, image, 0, 0)
-    all_sum(Copies(send, recv), at, total, result, land_core, land_x, land_plane)
-    result[...] = result[...] / count
-    factor_kernel(128, result.at[:, :order], inverse_ref, work, tile, pending)
-    inverse = inverse_ref[...]
-    basis = contract(slab, inverse, 1, 1)
-    basis_ref[...] = basis
-    projected = contract(product(inverse, result[:, order:]), inverse, 1, 1)
-    projected_ref[...] = projected
-    residual_ref[...] = contract(image, inverse, 1, 1) - product(basis, projected)
-
-
-def on_device(matrix, start_vectors, interval):
-    slab_rows, vectors = start_vectors.shape
-    total_rows = slab_rows * lax.axis_size("row") * lax.axis_size("col")
-    early, slab, mapped = filtered_blocks(matrix, start_vectors, interval)
-
-    f32 = jnp.float32
-    vmem = pl.BlockSpec(memory_space=pltpu.VMEM)
-    square = jax.ShapeDtypeStruct((vectors, vectors), f32)
-    tall = jax.ShapeDtypeStruct((slab_rows, vectors), f32)
-    cost = pl.CostEstimate(flops=2 * vectors**3, bytes_accessed=8 * vectors**2, transcendentals=vectors)
-    before = pl.pallas_call(
-        functools.partial(early_kernel, total_rows),
-        out_shape=square,
-        in_specs=[vmem],
-        out_specs=vmem,
-        scratch_shapes=sum_scratch(vectors, vectors),
-        compiler_params=pltpu.CompilerParams(collective_id=1, has_side_effects=True, vmem_limit_bytes=40 * 2**20),
-        cost_estimate=cost,
-    )(early)
-    return pl.pallas_call(
-        functools.partial(late_kernel, total_rows),
-        out_shape=(tall, square, tall),
-        in_specs=[vmem] * 3,
-        out_specs=(vmem,) * 3,
-        scratch_shapes=[pltpu.VMEM((vectors, vectors), f32)] + sum_scratch(vectors, 2 * vectors),
-        compiler_params=pltpu.CompilerParams(collective_id=2, has_side_effects=True, vmem_limit_bytes=40 * 2**20),
-        cost_estimate=cost,
-    )(slab, mapped, before)
 
 
 def solution(mesh):

time: 395 us -> 302 us (0.76)
  Pallas kernels: 389 us -> 296 us
    pallas_call x3 -> x1, Pallas kernels: 389 us -> 296 us  [on_device(): pl.pallas_call(functools.partial(whole_kernel, total_rows), out_shape=(ta...]
where the time goes in v5:
time: 302 us; the launch traced here: 301 us
  Pallas kernels  296 us (98%)
  local copies, waits for them, and re-layouts  4.52 us (1%)
    pallas_call x1, Pallas kernels, on_device(): pl.pallas_call(functools.partial(whole_kernel, total_rows), out_shape=(ta...  296 us

profile of v5, /device:TPU:1, one launch (start us, length us, event | category | flops | bytes accessed | tf_op | source)
XLA Modules:
  0.0 301.4 jit_solution(3385802488717058979)
XLA Ops:
  0.6 296.2 %shard_map.58 = (f32[64,512]{1,0:T(8,128)}, f32[512,512]{1,0:T(8,128)}, f32[64,512]{1,0:T(8,128)}) custom-call(f32[2]{0:T(128)} %interval_ref.1, f32[1024,512]{1,0:T(8,128)} %block_ref.1, f32[64,512]{1,0:T(8,128)} %start_ref.1), custom_call_target="tpu_custom_call" | custom-call | flops 10000000000 | bytes 4000000 | tf_op jit(solution)/shard_map/pallas_call | solution.py:636
  296.8 0.0 copy-start
  296.9 1.6 copy.9
  298.5 2.3 copy.10
  300.7 0.0 copy-done
  300.7 0.7 copy.11
Async XLA Ops:
  296.8 3.9 %copy-start = (f32[64,512]{1,0:T(8,128)S(1)}, f32[64,512]{1,0:T(8,128)}, u32[]{:S(2)}) copy-start(f32[64,512]{1,0:T(8,128)} %get-tuple-element.8) | copy-start | bytes 393220

commit v6 on v5

--- a/solution.py
+++ b/solution.py
@@ -9,7 +9,7 @@
 
 FILTER_DEG = 3
 OUTER = 2
-PANEL = 8
+PANEL = 16
 BLOCK = 128
 MESH = pl.DeviceIdType.MESH
 CHUNK = 128
@@ -31,7 +31,7 @@
 
 def lane_columns(rows, first):
     narrow = rows[:, :128]
-    lanes = jnp.zeros((PANEL, 128), jnp.int32) + first
+    lanes = jnp.zeros(narrow.shape, jnp.int32) + first
     return [jnp.take_along_axis(narrow, lanes + j, axis=1) for j in range(PANEL)]
 
 
@@ -39,7 +39,14 @@
     return jnp.broadcast_to(value[step : step + 1, :], value.shape)
 
 
-def factor_panels(tile, pending, begin, end):
+def three_parts(value):
+    high = value.astype(jnp.bfloat16).astype(jnp.float32)
+    rest = value - high
+    middle = rest.astype(jnp.bfloat16).astype(jnp.float32)
+    return high, middle, rest - middle
+
+
+def factor_panels(tile, pend_left, pend_right, begin, end):
     block = tile.shape[1] // 2
     sub = lax.broadcasted_iota(jnp.int32, (PANEL, 128), 0)
     lane = lax.broadcasted_iota(jnp.int32, (PANEL, block), 1)
@@ -48,8 +55,7 @@
         first = pl.multiple_of(p * PANEL, PANEL)
         here, after = pl.ds(first, PANEL), pl.ds(pl.multiple_of(first + PANEL, PANEL), PANEL)
         rows = tile[here, :]
-        late = pending[...]
-        tile[:block, :] -= contract(jnp.where(lane >= first + PANEL, late[:, :block], 0.0), late, 0, 0)
+        tile[:block, :] -= jnp.dot(pend_left[...], pend_right[...], preferred_element_type=jnp.float32)
 
         columns = lane_columns(rows, first)
         left, right = rows[:, :block], rows[:, block:]
@@ -67,6 +73,15 @@
                 left = left - ratio * row_of(left, s)
                 right = right - ratio * row_of(right, s)
 
+        scale = lax.rsqrt(pivots)
+        done_left, done_right = left * scale, right * scale
+        tile[here, :block] = done_left
+        tile[here, block:] = done_right
+        a = three_parts(jnp.where(lane >= first + 2 * PANEL, done_left, 0.0))
+        pend_left[...] = jnp.concatenate([a[0], a[0], a[1], a[1], a[0], a[2]], axis=0).T.astype(jnp.bfloat16)
+        b = three_parts(jnp.concatenate([done_left, done_right], axis=1))
+        pend_right[...] = jnp.concatenate([b[0], b[1], b[0], b[1], b[2], b[0]], axis=0).astype(jnp.bfloat16)
+
         following = tile[after, :]
         others = lane_columns(following, first)
         next_left, next_right = following[:, :block], following[:, block:]
@@ -78,18 +93,12 @@
             next_right = next_right - ratio * row_of(right, s)
         tile[after, :block] = next_left
         tile[after, block:] = next_right
-        scale = lax.rsqrt(pivots)
-        left, right = left * scale, right * scale
-        tile[here, :block] = left
-        tile[here, block:] = right
-        pending[:, :block] = left
-        pending[:, block:] = right
         return carry
 
     lax.fori_loop(begin, end, panel, 0)
 
 
-def factor_steps(pieces, work, inverse_ref, tile, pending):
+def factor_steps(pieces, work, inverse_ref, tile, pend_left, pend_right):
     order, block = work.shape[0], BLOCK
     at_row = lax.broadcasted_iota(jnp.int32, (order, order), 0)
     at_col = lax.broadcasted_iota(jnp.int32, (order, order), 1)
@@ -102,9 +111,10 @@
         tile[:block, :block] = work[at:stop, at:stop]
         tile[:block, block:] = (row == col).astype(jnp.float32)
         tile[block:, :] = jnp.zeros((PANEL, 2 * block), jnp.float32)
-        pending[...] = jnp.zeros_like(pending)
+        pend_left[...] = jnp.zeros_like(pend_left)
+        pend_right[...] = jnp.zeros_like(pend_right)
         for piece in range(pieces):
-            factor_panels(tile, pending, piece * panels // pieces, (piece + 1) * panels // pieces)
+            factor_panels(tile, pend_left, pend_right, piece * panels // pieces, (piece + 1) * panels // pieces)
             yield
         small = jnp.where(row >= col, tile[:block, block:], 0.0)
         solved = product(small, inverse_ref[at:stop, :stop])
@@ -211,7 +221,9 @@
     def one(a, b):
         return lax.dot_general(a, b, (dims, ((), ())), preferred_element_type=jnp.float32)
 
-    return one(left[0], right[0]) + (one(left[0], right[1]) + one(left[1], right[0]))
+    count = left.shape[0] // 2
+    both = one(left, right[0])
+    return both[:count] + (both[count:] + one(left[:count], right[1]))
 
 
 class TotalSum:
@@ -288,13 +300,13 @@
 
 def whole_kernel(
     count, interval_ref, block_ref, start_ref, basis_ref, projected_ref, residual_ref,
-    block, other, high, low, rows, row_parts, cols, col_parts, vec_high, vec_low,
+    block, other, high, low, rows, row_parts, cols, col_parts, vec,
     land_big, land_small, land_col, row_prev, col_prev, first_part,
     start_land, first_land, last_land, image_land, slab_ref, image_ref, before_ref, inverse_ref,
     *rest,
 ):
     sum_buffers = [rest[5 * k : 5 * k + 5] for k in range(3)]
-    tile, pending, send, recv, local_sem = rest[15:]
+    tile, pend_left, pend_right, send, recv, local_sem = rest[15:]
     r, c = lax.axis_index("row"), lax.axis_index("col")
     core, x, y, z = r % 2, r // 2, c % 4, c // 4
     copies = Copies(send, recv)
@@ -422,28 +434,26 @@
         def multiply(self):
             for q in range(4):
                 big, small = split(cols[q, self.all, :])
-                vec_high[self.all, q * CHUNK : (q + 1) * CHUNK] = big
-                vec_low[self.all, q * CHUNK : (q + 1) * CHUNK] = small
-
-            @pl.loop(0, 8)
+                vec[:share, q * CHUNK : (q + 1) * CHUNK] = big
+                vec[share:, q * CHUNK : (q + 1) * CHUNK] = small
+
+            @pl.loop(0, 8, unroll=4)
             def _(i):
                 at = pl.ds(pl.multiple_of(i * 256, 256), 256)
-                left = vec_high[self.all, :], vec_low[self.all, :]
-                out = three_pass(left, (high[at, :], low[at, :]), ((1,), (1,)))
+                out = three_pass(vec[...], (high[at, :], low[at, :]), ((1,), (1,)))
                 row_parts[i // 2, 2 * (i % 2), self.all, :] = out[:, :CHUNK]
                 row_parts[i // 2, 2 * (i % 2) + 1, self.all, :] = out[:, CHUNK:]
 
         def multiply_turned(self):
+            def one(i):
+                at = pl.ds(pl.multiple_of(i * 1024, 1024), 1024)
+                wide = jnp.concatenate([rows[2 * i + k // 4, k % 4, self.all, :] for k in range(8)], axis=1)
+                left = jnp.concatenate(split(wide), axis=0)
+                return three_pass(left, (high[at, :], low[at, :]), ((1,), (0,)))
+
+            out = one(0) + one(1)
             for q in range(4):
-                col_parts[q, self.all, :] = jnp.zeros((share, CHUNK), jnp.float32)
-
-            @pl.loop(0, 8)
-            def _(i):
-                at = pl.ds(pl.multiple_of(i * 256, 256), 256)
-                pair = [rows[i // 2, 2 * (i % 2) + k, self.all, :] for k in range(2)]
-                out = three_pass(split(jnp.concatenate(pair, axis=1)), (high[at, :], low[at, :]), ((1,), (0,)))
-                for q in range(4):
-                    col_parts[q, self.all, :] += out[:, q * CHUNK : (q + 1) * CHUNK]
+                col_parts[q, self.all, :] = out[:, q * CHUNK : (q + 1) * CHUNK]
 
         def to_rows(self):
             self.multiply()
@@ -545,7 +555,7 @@
         sums[0].total[...] = contract(slab_ref[...], slab_ref[...], 0, 0)
         yield from sums[0].steps()
         sums[0].total[...] = sums[0].result[...] / count
-        yield from factor_steps(2, sums[0].total, before_ref, tile, pending)
+        yield from factor_steps(2, sums[0].total, before_ref, tile, pend_left, pend_right)
 
     def last_chain():
         yield from trade(col_prev[...], last_land, slab_ref)
@@ -553,7 +563,7 @@
         sums[1].total[...] = contract(slab_ref[...], slab_ref[...], 0, 0)
         yield from sums[1].steps()
         sums[1].total[...] = sums[1].result[...] / count
-        yield from factor_steps(2, sums[1].total, inverse_ref, tile, pending)
+        yield from factor_steps(2, sums[1].total, inverse_ref, tile, pend_left, pend_right)
 
     def image_chain():
         image_land[2, :, :] = row_parts[y, z].T
@@ -647,8 +657,7 @@
             pltpu.VMEM((4, 4, width, CHUNK), f32),
             pltpu.VMEM((4, width, CHUNK), f32),
             pltpu.VMEM((4, width, CHUNK), f32),
-            pltpu.VMEM((width, block_cols), bf16),
-            pltpu.VMEM((width, block_cols), bf16),
+            pltpu.VMEM((2 * share, block_cols), bf16),
             pltpu.VMEM((STREAMS, 2, 6, 4, share // 4, CHUNK), f32),
             pltpu.VMEM((STREAMS, 2, 6, share // 4, CHUNK), f32),
             pltpu.VMEM((STREAMS, 6, share // 2, CHUNK), f32),
@@ -665,7 +674,8 @@
             pltpu.VMEM((vectors, vectors), f32),
             *(one_sum * 3),
             pltpu.VMEM((BLOCK + PANEL, 2 * BLOCK), f32),
-            pltpu.VMEM((PANEL, 2 * BLOCK), f32),
+            pltpu.VMEM((BLOCK, 6 * PANEL), bf16),
+            pltpu.VMEM((6 * PANEL, 2 * BLOCK), bf16),
             pltpu.SemaphoreType.DMA((256,)),
             pltpu.SemaphoreType.DMA((256,)),
             pltpu.SemaphoreType.DMA,

time: 302 us -> 274 us (0.907)
  Pallas kernels: 296 us -> 269 us
    pallas_call x1, Pallas kernels: 296 us -> 269 us  [on_device(): pl.pallas_call(functools.partial(whole_kernel, total_rows), out_shape=(ta...]
where the time goes in v6:
time: 274 us
  Pallas kernels  269 us (98%)
  local copies, waits for them, and re-layouts  4.52 us (2%)
    pallas_call x1, Pallas kernels, on_device(): pl.pallas_call(functools.partial(whole_kernel, total_rows), out_shape=(ta...  269 us

profile of v6, /device:TPU:1, one launch (start us, length us, event | category | flops | bytes accessed | tf_op | source)
XLA Modules:
  0.0 274.3 jit_solution(10696565914432764244)
XLA Ops:
  0.6 269.1 %shard_map.58 = (f32[64,512]{1,0:T(8,128)}, f32[512,512]{1,0:T(8,128)}, f32[64,512]{1,0:T(8,128)}) custom-call(f32[2]{0:T(128)} %interval_ref.1, f32[1024,512]{1,0:T(8,128)} %block_ref.1, f32[64,512]{1,0:T(8,128)} %start_ref.1), custom_call_target="tpu_custom_call" | custom-call | flops 10000000000 | bytes 4000000 | tf_op jit(solution)/shard_map/pallas_call | solution.py:646
  269.8 0.0 copy-start
  269.8 1.6 copy.9
  271.4 2.3 copy.10
  273.7 0.0 copy-done
  273.7 0.7 copy.11
Async XLA Ops:
  269.8 3.9 %copy-start = (f32[64,512]{1,0:T(8,128)S(1)}, f32[64,512]{1,0:T(8,128)}, u32[]{:S(2)}) copy-start(f32[64,512]{1,0:T(8,128)} %get-tuple-element.8) | copy-start | bytes 393220

commit v7 on v6

--- a/solution.py
+++ b/solution.py
@@ -227,36 +227,29 @@
 
 
 class TotalSum:
-    def __init__(self, copies, position, mate, ring_x, peers, buffers):
+    def __init__(self, copies, position, mate, peers, x_peers, buffers):
         core, x, c = position
-        self.total, self.result, self.land_core, land_x, self.land_plane = buffers
-        order, width = self.total.shape
-        half, quarter = order // 2, order // 8
+        self.x = x
+        self.total, self.result, self.land_core, self.land_plane, self.land_x = buffers
+        half = self.total.shape[0] // 2
+        size = half // 16
 
         def rows(ref, first, count):
-            return ref.at[pl.ds(pl.multiple_of(first, 8), count), :]
-
-        def part(ref):
-            def one(t, side):
-                size = quarter if side is None else quarter // 2
-                return rows(ref, core * half + t * quarter + (0 if side is None else side * size), size)
-            return one
+            return ref.at[pl.ds(pl.multiple_of(first, size), count), :]
 
         def piece(ref, t):
-            first = core * half + x * quarter + 8 * (t // 2)
-            lanes = pl.ds(pl.multiple_of((t % 2) * (width // 2), 128), width // 2)
-            return ref.at[pl.ds(pl.multiple_of(first, 8), 8), lanes]
+            return rows(ref, core * half + t * size, size)
 
         self.mine = rows(self.total, core * half, half)
         self.swap = copies.make(rows(self.total, (1 - core) * half, half), self.land_core, copies.reserve(1), mate)
-        self.scatter = Scatter(copies, copies.reserve(6), x, ring_x, part(self.total), lambda i: land_x.at[i])
         self.own, self.summed = piece(self.total, c), piece(self.result, c)
-        self.there, self.back = [], []
+        self.there, self.along, self.back = [], [], []
         for offset, peer in peers:
             source, target = piece(self.total, (c + offset) % 16), self.land_plane.at[offset]
             self.there.append(copies.make(source, target, copies.reserve(1), peer))
             self.back.append(copies.make(self.summed, self.summed, copies.reserve(1), peer))
-        self.gather = Gather(copies, copies.reserve(4), x, ring_x, part(self.result))
+        for offset, peer in x_peers:
+            self.along.append(copies.make(self.land_x.at[0], self.land_x.at[offset], copies.reserve(1), peer))
         whole = rows(self.result, core * half, half)
         self.give = copies.make(whole, whole, copies.reserve(1), mate)
 
@@ -265,11 +258,6 @@
         yield
         self.swap.wait_recv()
         self.mine[...] += self.land_core[...]
-        self.scatter.start()
-        yield
-        self.scatter.relay()
-        yield
-        self.scatter.finish()
         for copy in self.there:
             copy.start()
         yield
@@ -277,19 +265,23 @@
         for offset, copy in enumerate(self.there, 1):
             copy.wait_recv()
             value = value + self.land_plane[offset]
+        self.land_x[0] = value
+        for copy in self.along:
+            copy.start()
+        yield
+        for copy in self.along:
+            copy.wait_recv()
+        value = self.land_x[self.x % 4]
+        for at in range(1, 4):
+            value = value + self.land_x[(self.x + 4 - at) % 4]
         self.summed[...] = value
         for copy in self.back:
             copy.start()
         yield
         for copy in self.back:
             copy.wait_recv()
-        self.gather.start()
-        yield
-        self.gather.forward()
-        yield
-        self.gather.finish()
         self.give.start()
-        for copy in (self.swap, *self.there, *self.back):
+        for copy in (self.swap, *self.there, *self.along, *self.back):
             copy.wait_send()
         yield
         self.give.wait()
@@ -328,7 +320,8 @@
         pl.semaphore_signal(barrier, inc=1, device_id=who, device_id_type=MESH)
 
     peers = [(offset, (r, (c + offset) % 16)) for offset in range(1, 16)]
-    for who in (mate, *ring_x, *(peer for _, peer in peers)):
+    x_peers = [(offset, ((r + 2 * offset) % 8, c)) for offset in range(1, 4)]
+    for who in (mate, *(peer for _, peer in x_peers), *(peer for _, peer in peers)):
         greet(who)
 
     @pl.when(crossed)
@@ -336,7 +329,7 @@
         greet(device(z, core, y, x))
         greet(device(z, 1 - core, y, x))
 
-    pl.semaphore_wait(barrier, jnp.where(crossed, 20, 18))
+    pl.semaphore_wait(barrier, jnp.where(crossed, 21, 19))
 
     block_rows, block_cols = block.shape
     slab = start_ref.shape[0]
@@ -539,7 +532,7 @@
     keep = pl.ds(pl.multiple_of(core * slab, slab), slab)
     give = pl.ds(pl.multiple_of((1 - core) * slab, slab), slab)
     top = pl.ds(0, slab)
-    sums = [TotalSum(copies, (core, x, c), mate, ring_x, peers, buffers) for buffers in sum_buffers]
+    sums = [TotalSum(copies, (core, x, c), mate, peers, x_peers, buffers) for buffers in sum_buffers]
 
     def trade(piece, land, target):
         land[1] = piece.T
@@ -564,6 +557,7 @@
         yield from sums[1].steps()
         sums[1].total[...] = sums[1].result[...] / count
         yield from factor_steps(2, sums[1].total, inverse_ref, tile, pend_left, pend_right)
+        basis_ref[...] = contract(slab_ref[...], inverse_ref[...], 1, 1)
 
     def image_chain():
         image_land[2, :, :] = row_parts[y, z].T
@@ -614,13 +608,15 @@
     while len(chains) > 1:
         if not advance(chains[0]):
             chains.pop(0)
-    chains.append(image_chain())
-    while chains:
-        chains = [chain for chain in reversed(chains) if advance(chain)][::-1]
+    image = image_chain()
+    ending, closing = True, True
+    while ending or closing:
+        ending = ending and advance(image)
+        for _ in range(2):
+            closing = closing and advance(chains[0])
 
     inverse = inverse_ref[...]
-    basis = contract(slab_ref[...], inverse, 1, 1)
-    basis_ref[...] = basis
+    basis = basis_ref[...]
     projected = contract(product(inverse, sums[2].result[...] / count), inverse, 1, 1)
     projected_ref[...] = projected
     residual_ref[...] = contract(image_ref[...], inverse, 1, 1) - product(basis, projected)
@@ -640,8 +636,8 @@
         pltpu.VMEM((vectors, vectors), f32),
         pltpu.VMEM((vectors, vectors), f32),
         pltpu.VMEM((vectors // 2, vectors), f32),
-        pltpu.VMEM((6, vectors // 16, vectors), f32),
-        pltpu.VMEM((16, 8, vectors // 2), f32),
+        pltpu.VMEM((16, vectors // 32, vectors), f32),
+        pltpu.VMEM((4, vectors // 32, vectors), f32),
     ]
     return pl.pallas_call(
         functools.partial(whole_kernel, total_rows),

time: 274 us -> 272 us (level)
  no operation moved by 1% of the time
where the time goes in v7:
time: 272 us
  Pallas kernels  267 us (98%)
  local copies, waits for them, and re-layouts  4.52 us (2%)
    pallas_call x1, Pallas kernels, on_device(): pl.pallas_call(functools.partial(whole_kernel, total_rows), out_shape=(ta...  267 us

profile of v7, /device:TPU:1, one launch (start us, length us, event | category | flops | bytes accessed | tf_op | source)
XLA Modules:
  0.0 272.2 jit_solution(17812057609555102089)
XLA Ops:
  0.6 267.1 %shard_map.58 = (f32[64,512]{1,0:T(8,128)}, f32[512,512]{1,0:T(8,128)}, f32[64,512]{1,0:T(8,128)}) custom-call(f32[2]{0:T(128)} %interval_ref.1, f32[1024,512]{1,0:T(8,128)} %block_ref.1, f32[64,512]{1,0:T(8,128)} %start_ref.1), custom_call_target="tpu_custom_call" | custom-call | flops 10000000000 | bytes 4000000 | tf_op jit(solution)/shard_map/pallas_call | solution.py:642
  267.7 0.0 copy-start
  267.7 1.6 copy.9
  269.3 2.3 copy.10
  271.6 0.0 copy-done
  271.6 0.7 copy.11
Async XLA Ops:
  267.7 3.9 %copy-start = (f32[64,512]{1,0:T(8,128)S(1)}, f32[64,512]{1,0:T(8,128)}, u32[]{:S(2)}) copy-start(f32[64,512]{1,0:T(8,128)} %get-tuple-element.8) | copy-start | bytes 393220

commit v8 on v7

--- a/solution.py
+++ b/solution.py
@@ -147,9 +147,11 @@
 
 
 class Scatter:
+    relays = True
+
     def __init__(self, copies, slot, place, ring, part, land):
         self.place, self.part, self.land = place, part, land
-        left, right = ring
+        left, right = ring[3], ring[1]
         ahead, behind, across = (place + 1) % 4, (place + 3) % 4, (place + 2) % 4
         self.ahead, self.behind = ahead, behind
         plan = (
@@ -186,8 +188,10 @@
 
 
 class Gather:
+    relays = True
+
     def __init__(self, copies, slot, place, ring, part):
-        left, right = ring
+        left, right = ring[3], ring[1]
         ahead, behind = (place + 1) % 4, (place + 3) % 4
         self.copies = [
             copies.make(part(place, None), part(place, None), slot, right),
@@ -207,6 +211,46 @@
 
     def finish(self):
         for copy in self.copies[2:]:
+            copy.wait_recv()
+        for copy in self.copies:
+            copy.wait_send()
+
+
+class DirectScatter:
+    relays = False
+
+    def __init__(self, copies, slot, place, ring, part, land):
+        self.mine, self.land = part(place, None), land
+        self.copies = [
+            copies.make(part((place + offset) % 4, None), land(offset - 1), slot + offset - 1, ring[offset])
+            for offset in (2, 1, 3)
+        ]
+
+    def start(self):
+        for copy in self.copies:
+            copy.start()
+
+    def finish(self):
+        for copy in self.copies:
+            copy.wait_recv()
+        self.mine[...] += self.land(0)[...] + (self.land(1)[...] + self.land(2)[...])
+        for copy in self.copies:
+            copy.wait_send()
+
+
+class DirectGather:
+    relays = False
+
+    def __init__(self, copies, slot, place, ring, part):
+        own = part(place, None)
+        self.copies = [copies.make(own, own, slot + offset - 1, ring[offset]) for offset in (2, 1, 3)]
+
+    def start(self):
+        for copy in self.copies:
+            copy.start()
+
+    def finish(self):
+        for copy in self.copies:
             copy.wait_recv()
         for copy in self.copies:
             copy.wait_send()
@@ -288,6 +332,9 @@
 
 
 STREAMS = 2
+LEAD = 0
+SCATTERS = (Scatter, DirectScatter, DirectScatter)
+GATHERS = (DirectGather, Gather, DirectGather)
 
 
 def whole_kernel(
@@ -307,9 +354,9 @@
         return (2 * x + core, 4 * z + y)
 
     mate = device(x, 1 - core, y, z)
-    ring_x = device((x + 3) % 4, core, y, z), device((x + 1) % 4, core, y, z)
-    ring_y = device(x, core, (y + 3) % 4, z), device(x, core, (y + 1) % 4, z)
-    ring_z = device(x, core, y, (z + 3) % 4), device(x, core, y, (z + 1) % 4)
+    ring_x = {offset: device((x + offset) % 4, core, y, z) for offset in (1, 2, 3)}
+    ring_y = {offset: device(x, core, (y + offset) % 4, z) for offset in (1, 2, 3)}
+    ring_z = {offset: device(x, core, y, (z + offset) % 4) for offset in (1, 2, 3)}
     crossed = x != z
 
     local = pltpu.make_async_copy(block_ref, block, local_sem)
@@ -320,7 +367,7 @@
         pl.semaphore_signal(barrier, inc=1, device_id=who, device_id_type=MESH)
 
     peers = [(offset, (r, (c + offset) % 16)) for offset in range(1, 16)]
-    x_peers = [(offset, ((r + 2 * offset) % 8, c)) for offset in range(1, 4)]
+    x_peers = list(ring_x.items())
     for who in (mate, *(peer for _, peer in x_peers), *(peer for _, peer in peers)):
         greet(who)
 
@@ -387,10 +434,10 @@
             self.scatters = [[self.scatter(index, u, stage, slots[u][stage]) for stage in range(2)] for u in range(2)]
             slots = [[copies.reserve(4) for _ in range(2)] for _ in range(2)]
             self.gathers = [[self.gather(u, stage, slots[u][stage]) for stage in range(2)] for u in range(2)]
-            self.col_scatter = Scatter(
+            self.col_scatter = SCATTERS[2](
                 copies, copies.reserve(6), x, ring_x, self.col_slice(col_parts), lambda i: land_col.at[index, i]
             )
-            self.col_gather = Gather(copies, copies.reserve(4), x, ring_x, self.col_slice(cols))
+            self.col_gather = GATHERS[2](copies, copies.reserve(4), x, ring_x, self.col_slice(cols))
 
         def span(self, colour, side):
             size = half if side is None else half // 2
@@ -417,12 +464,12 @@
             axis = orders[colour][stage]
             part = (self.plane if stage == 0 else self.line)(row_parts, colour, axis)
             landing = land_big if stage == 0 else land_small
-            return Scatter(copies, slot, places[axis], rings[axis], part, lambda i: landing.at[index, colour, i])
+            return SCATTERS[stage](copies, slot, places[axis], rings[axis], part, lambda i: landing.at[index, colour, i])
 
         def gather(self, colour, stage, slot):
             axis = orders[colour][1 - stage]
             part = (self.line if stage == 0 else self.plane)(rows, colour, axis)
-            return Gather(copies, slot, places[axis], rings[axis], part)
+            return GATHERS[stage](copies, slot, places[axis], rings[axis], part)
 
         def multiply(self):
             for q in range(4):
@@ -455,62 +502,72 @@
             for first in firsts:
                 first.start()
             yield
-            for first in firsts:
-                first.relay()
-            yield
+            if firsts[0].relays:
+                for first in firsts:
+                    first.relay()
+                yield
             for first, second in zip(firsts, seconds):
                 first.finish()
                 second.start()
             yield
-            for second in seconds:
-                second.relay()
+            if seconds[0].relays:
+                for second in seconds:
+                    second.relay()
+                yield
+
+        def gather_rows(self, step):
+            for colour in range(2):
+                self.scatters[colour][1].finish()
+                at = self.span(colour, None)
+                value = row_parts[y, z, at, :]
+                if step > 0:
+                    value = 2.0 * value - row_prev[at, :]
+                rows[y, z, at, :] = value
+                row_prev[at, :] = value
+                if step == 1:
+                    first_part[at, :] = value
+                self.gathers[colour][0].start()
+            self.at_first = step >= 1
             yield
+            for stage in range(2):
+                pair = [self.gathers[0][stage], self.gathers[1][stage]]
+                if pair[0].relays:
+                    for one in pair:
+                        one.forward()
+                    yield
+                for colour in range(2):
+                    pair[colour].finish()
+                    if stage == 0:
+                        self.gathers[colour][1].start()
+                if stage == 0:
+                    yield
+
+        def to_cols(self, step):
+            self.multiply_turned()
+            self.col_scatter.start()
+            yield
+            if self.col_scatter.relays:
+                self.col_scatter.relay()
+                yield
+            self.col_scatter.finish()
+            value = col_parts[x, self.all, :]
+            if step != 1:
+                value = 2.0 * value - col_prev[self.all, :]
+            cols[x, self.all, :] = value
+            col_prev[self.all, :] = value
+            self.col_gather.start()
+            self.at_last = step == 2
+            yield
+            if self.col_gather.relays:
+                self.col_gather.forward()
+                yield
+            self.col_gather.finish()
 
         def run(self):
             for step in range(3):
                 yield from self.to_rows()
-                for colour in range(2):
-                    self.scatters[colour][1].finish()
-                    at = self.span(colour, None)
-                    value = row_parts[y, z, at, :]
-                    if step > 0:
-                        value = 2.0 * value - row_prev[at, :]
-                    rows[y, z, at, :] = value
-                    row_prev[at, :] = value
-                    if step == 1:
-                        first_part[at, :] = value
-                    self.gathers[colour][0].start()
-                self.at_first = step >= 1
-                yield
-                for colour in range(2):
-                    self.gathers[colour][0].forward()
-                yield
-                for colour in range(2):
-                    self.gathers[colour][0].finish()
-                    self.gathers[colour][1].start()
-                yield
-                for colour in range(2):
-                    self.gathers[colour][1].forward()
-                yield
-                for colour in range(2):
-                    self.gathers[colour][1].finish()
-                self.multiply_turned()
-                self.col_scatter.start()
-                yield
-                self.col_scatter.relay()
-                yield
-                self.col_scatter.finish()
-                value = col_parts[x, self.all, :]
-                if step != 1:
-                    value = 2.0 * value - col_prev[self.all, :]
-                cols[x, self.all, :] = value
-                col_prev[self.all, :] = value
-                self.col_gather.start()
-                self.at_last = step == 2
-                yield
-                self.col_gather.forward()
-                yield
-                self.col_gather.finish()
+                yield from self.gather_rows(step)
+                yield from self.to_cols(step)
             yield from self.to_rows()
             for colour in range(2):
                 self.scatters[colour][1].finish()
@@ -521,7 +578,8 @@
     local.wait()
     prepare(block, core)
     for stream in streams:
-        stream.col_gather.forward()
+        if stream.col_gather.relays:
+            stream.col_gather.forward()
     start_copy.wait_send()
     block_copy.wait_recv()
     prepare(other, 1 - core)
@@ -592,6 +650,8 @@
 
     runs = [stream.run() for stream in streams]
     chains, begun = [], 0
+    for _ in range(LEAD):
+        advance(runs[0])
     going = True
     while going:
         going = False
@@ -655,8 +715,8 @@
             pltpu.VMEM((4, width, CHUNK), f32),
             pltpu.VMEM((2 * share, block_cols), bf16),
             pltpu.VMEM((STREAMS, 2, 6, 4, share // 4, CHUNK), f32),
-            pltpu.VMEM((STREAMS, 2, 6, share // 4, CHUNK), f32),
-            pltpu.VMEM((STREAMS, 6, share // 2, CHUNK), f32),
+            pltpu.VMEM((STREAMS, 2, 3, share // 2, CHUNK), f32),
+            pltpu.VMEM((STREAMS, 3, share, CHUNK), f32),
             pltpu.VMEM((width, CHUNK), f32),
             pltpu.VMEM((width, CHUNK), f32),
             pltpu.VMEM((width, CHUNK), f32),

time: 272 us -> 241 us (0.89)
  Pallas kernels: 267 us -> 236 us
    pallas_call x1, Pallas kernels: 267 us -> 236 us  [on_device(): pl.pallas_call(functools.partial(whole_kernel, total_rows), out_shape=(ta...]
where the time goes in v8:
time: 241 us
  Pallas kernels  236 us (98%)
  local copies, waits for them, and re-layouts  4.52 us (2%)
    pallas_call x1, Pallas kernels, on_device(): pl.pallas_call(functools.partial(whole_kernel, total_rows), out_shape=(ta...  236 us

profile of v8, /device:TPU:1, one launch (start us, length us, event | category | flops | bytes accessed | tf_op | source)
XLA Modules:
  0.0 241.1 jit_solution(482523968476834448)
XLA Ops:
  0.6 235.9 %shard_map.58 = (f32[64,512]{1,0:T(8,128)}, f32[512,512]{1,0:T(8,128)}, f32[64,512]{1,0:T(8,128)}) custom-call(f32[2]{0:T(128)} %interval_ref.1, f32[1024,512]{1,0:T(8,128)} %block_ref.1, f32[64,512]{1,0:T(8,128)} %start_ref.1), custom_call_target="tpu_custom_call" | custom-call | flops 10000000000 | bytes 4000000 | tf_op jit(solution)/shard_map/pallas_call | solution.py:702
  236.5 0.0 copy-start
  236.5 1.6 copy.9
  238.1 2.3 copy.10
  240.4 0.0 copy-done
  240.4 0.7 copy.11
Async XLA Ops:
  236.5 3.9 %copy-start = (f32[64,512]{1,0:T(8,128)S(1)}, f32[64,512]{1,0:T(8,128)}, u32[]{:S(2)}) copy-start(f32[64,512]{1,0:T(8,128)} %get-tuple-element.8) | copy-start | bytes 393220

commit v9 on v8

--- a/solution.py
+++ b/solution.py
@@ -11,6 +11,7 @@
 OUTER = 2
 PANEL = 16
 BLOCK = 128
+WORK = "work"
 MESH = pl.DeviceIdType.MESH
 CHUNK = 128
 
@@ -115,7 +116,7 @@
         pend_right[...] = jnp.zeros_like(pend_right)
         for piece in range(pieces):
             factor_panels(tile, pend_left, pend_right, piece * panels // pieces, (piece + 1) * panels // pieces)
-            yield
+            yield WORK
         small = jnp.where(row >= col, tile[:block, block:], 0.0)
         solved = product(small, inverse_ref[at:stop, :stop])
         inverse_ref[at:stop, :stop] = solved
@@ -123,7 +124,7 @@
             below = contract(work[stop:, at:stop], small, 1, 1)
             work[stop:, stop:] -= contract(below, below, 1, 1)
             inverse_ref[stop:, :stop] -= product(below, solved)
-            yield
+            yield WORK
 
 
 class Copies:
@@ -332,7 +333,7 @@
 
 
 STREAMS = 2
-LEAD = 0
+PIECES_A_WAIT = 3
 SCATTERS = (Scatter, DirectScatter, DirectScatter)
 GATHERS = (DirectGather, Gather, DirectGather)
 
@@ -645,35 +646,38 @@
         sums[2].total[...] = contract(slab_ref[...], image_ref[...], 0, 0)
         yield from sums[2].steps()
 
-    def advance(chain):
-        return next(chain, "end") != "end"
-
-    runs = [stream.run() for stream in streams]
+    class Chain:
+        def __init__(self, steps):
+            self.steps, self.ready, self.ended = steps, False, False
+
+        def advance(self):
+            if not self.ended:
+                said = next(self.steps, "end")
+                self.ready, self.ended = said == WORK, said == "end"
+
+    runs = [Chain(stream.run()) for stream in streams]
     chains, begun = [], 0
-    for _ in range(LEAD):
-        advance(runs[0])
-    going = True
-    while going:
-        going = False
-        for run in runs:
-            going = advance(run) or going
-            if chains and not advance(chains[0]):
-                chains.pop(0)
+    while not all(run.ended for run in runs):
+        for index, run in enumerate(runs):
+            run.advance()
+            if chains and (chains[0].ready or index == len(runs) - 1):
+                chains[0].advance()
+                if chains[0].ended:
+                    chains.pop(0)
         if begun == 0 and all(stream.at_first for stream in streams):
-            chains.append(first_chain())
+            chains.append(Chain(first_chain()))
             begun = 1
         if begun == 1 and all(stream.at_last for stream in streams):
-            chains.append(last_chain())
+            chains.append(Chain(last_chain()))
             begun = 2
-    while len(chains) > 1:
-        if not advance(chains[0]):
-            chains.pop(0)
-    image = image_chain()
-    ending, closing = True, True
-    while ending or closing:
-        ending = ending and advance(image)
-        for _ in range(2):
-            closing = closing and advance(chains[0])
+    image = Chain(image_chain())
+    while chains or not image.ended:
+        image.advance()
+        for turn in range(PIECES_A_WAIT):
+            if chains and (chains[0].ready or turn == 0 or image.ended):
+                chains[0].advance()
+                if chains[0].ended:
+                    chains.pop(0)
 
     inverse = inverse_ref[...]
     basis = basis_ref[...]

time: 241 us -> 227 us (0.942)
  Pallas kernels: 236 us -> 221 us
    pallas_call x1, Pallas kernels: 236 us -> 221 us  [on_device(): pl.pallas_call(functools.partial(whole_kernel, total_rows), out_shape=(ta...]
where the time goes in v9:
time: 227 us; the launch traced here: 226 us
  Pallas kernels  221 us (97%)
  local copies, waits for them, and re-layouts  4.52 us (2%)
    pallas_call x1, Pallas kernels, on_device(): pl.pallas_call(functools.partial(whole_kernel, total_rows), out_shape=(ta...  221 us

profile of v9, /device:TPU:1, one launch (start us, length us, event | category | flops | bytes accessed | tf_op | source)
XLA Modules:
  0.0 226.0 jit_solution(3069465627216575257)
XLA Ops:
  0.6 220.8 %shard_map.58 = (f32[64,512]{1,0:T(8,128)}, f32[512,512]{1,0:T(8,128)}, f32[64,512]{1,0:T(8,128)}) custom-call(f32[2]{0:T(128)} %interval_ref.1, f32[1024,512]{1,0:T(8,128)} %block_ref.1, f32[64,512]{1,0:T(8,128)} %start_ref.1), custom_call_target="tpu_custom_call" | custom-call | flops 10000000000 | bytes 4000000 | tf_op jit(solution)/shard_map/pallas_call | solution.py:706
  221.4 0.0 copy-start
  221.5 1.6 copy.9
  223.1 2.3 %copy.10 = f32[512,512]{1,0:T(8,128)} copy(f32[512,512]{1,0:T(8,128)} %get-tuple-element.7) | data formatting | bytes 2097152
  225.3 0.0 copy-done
  225.3 0.7 copy.11
Async XLA Ops:
  221.4 3.9 %copy-start = (f32[64,512]{1,0:T(8,128)S(1)}, f32[64,512]{1,0:T(8,128)}, u32[]{:S(2)}) copy-start(f32[64,512]{1,0:T(8,128)} %get-tuple-element.8) | copy-start | bytes 393220

commit v10 on v9

--- a/solution.py
+++ b/solution.py
@@ -275,22 +275,17 @@
     def __init__(self, copies, position, mate, peers, x_peers, buffers):
         core, x, c = position
         self.x = x
-        self.total, self.result, self.land_core, self.land_plane, self.land_x = buffers
-        half = self.total.shape[0] // 2
+        self.total, self.result, self.land_plane, self.land_x = buffers
+        half = self.total.shape[0]
         size = half // 16
 
         def rows(ref, first, count):
             return ref.at[pl.ds(pl.multiple_of(first, size), count), :]
 
-        def piece(ref, t):
-            return rows(ref, core * half + t * size, size)
-
-        self.mine = rows(self.total, core * half, half)
-        self.swap = copies.make(rows(self.total, (1 - core) * half, half), self.land_core, copies.reserve(1), mate)
-        self.own, self.summed = piece(self.total, c), piece(self.result, c)
+        self.own, self.summed = rows(self.total, c * size, size), rows(self.result, core * half + c * size, size)
         self.there, self.along, self.back = [], [], []
         for offset, peer in peers:
-            source, target = piece(self.total, (c + offset) % 16), self.land_plane.at[offset]
+            source, target = rows(self.total, (c + offset) % 16 * size, size), self.land_plane.at[offset]
             self.there.append(copies.make(source, target, copies.reserve(1), peer))
             self.back.append(copies.make(self.summed, self.summed, copies.reserve(1), peer))
         for offset, peer in x_peers:
@@ -299,10 +294,6 @@
         self.give = copies.make(whole, whole, copies.reserve(1), mate)
 
     def steps(self):
-        self.swap.start()
-        yield
-        self.swap.wait_recv()
-        self.mine[...] += self.land_core[...]
         for copy in self.there:
             copy.start()
         yield
@@ -326,7 +317,7 @@
         for copy in self.back:
             copy.wait_recv()
         self.give.start()
-        for copy in (self.swap, *self.there, *self.along, *self.back):
+        for copy in (*self.there, *self.along, *self.back):
             copy.wait_send()
         yield
         self.give.wait()
@@ -345,8 +336,8 @@
     start_land, first_land, last_land, image_land, slab_ref, image_ref, before_ref, inverse_ref,
     *rest,
 ):
-    sum_buffers = [rest[5 * k : 5 * k + 5] for k in range(3)]
-    tile, pend_left, pend_right, send, recv, local_sem = rest[15:]
+    sum_buffers = [rest[4 * k : 4 * k + 4] for k in range(3)]
+    tile, pend_left, pend_right, send, recv, local_sem = rest[12:]
     r, c = lax.axis_index("row"), lax.axis_index("col")
     core, x, y, z = r % 2, r // 2, c % 4, c // 4
     copies = Copies(send, recv)
@@ -369,7 +360,8 @@
 
     peers = [(offset, (r, (c + offset) % 16)) for offset in range(1, 16)]
     x_peers = list(ring_x.items())
-    for who in (mate, *(peer for _, peer in x_peers), *(peer for _, peer in peers)):
+    across = {offset: device((x + offset) % 4, 1 - core, y, z) for offset in range(4)}
+    for who in (*across.values(), *(peer for _, peer in x_peers), *(peer for _, peer in peers)):
         greet(who)
 
     @pl.when(crossed)
@@ -377,18 +369,13 @@
         greet(device(z, core, y, x))
         greet(device(z, 1 - core, y, x))
 
-    pl.semaphore_wait(barrier, jnp.where(crossed, 21, 19))
-
     block_rows, block_cols = block.shape
     slab = start_ref.shape[0]
     width = start_ref.shape[1] // 2
+    share = width // STREAMS
+    half = share // 2
     mine_cols = pl.ds(pl.multiple_of(core * width, width), width)
     mate_cols = pl.ds(pl.multiple_of((1 - core) * width, width), width)
-
-    start_copy = copies.make(start_ref.at[:, mate_cols], start_land, copies.reserve(1), mate)
-    start_copy.start()
-    block_copy = copies.make(block_ref, other, copies.reserve(1), mate)
-    block_copy.start()
 
     lower_end = jnp.full((1, block_cols), interval_ref[0], jnp.float32)
     upper_end = jnp.full((1, block_cols), interval_ref[1], jnp.float32)
@@ -411,20 +398,31 @@
             high[to, :] = big
             low[to, :] = small
 
-    start_copy.wait_recv()
-    own = start_ref[:, mine_cols]
-    theirs = start_land[...]
-    lower = jnp.where(core == 0, own, theirs)
-    upper = jnp.where(core == 0, theirs, own)
-    piece = jnp.concatenate([lower, upper], axis=0).T
-    cols[x] = piece
-    col_prev[...] = piece
+    local.wait()
+    prepare(block, core)
+    start_land[r] = start_ref[:, mine_cols]
+    pl.semaphore_wait(barrier, jnp.where(crossed, 24, 22))
+
+    start_copies = []
+    for index in range(STREAMS):
+        lanes = pl.ds(index * share, share)
+        own = start_ref.at[:, pl.ds(pl.multiple_of(core * width + index * share, share), share)]
+        theirs = start_ref.at[:, pl.ds(pl.multiple_of((1 - core) * width + index * share, share), share)]
+        ways = [(theirs, across[0])]
+        for offset in (2, 1, 3):
+            ways += [(own, ring_x[offset]), (theirs, across[offset])]
+        start_copies.append([
+            copies.make(source, start_land.at[r, :, lanes], copies.reserve(1), peer) for source, peer in ways
+        ])
+    for group in start_copies:
+        for copy in group:
+            copy.start()
+    block_copy = copies.make(block_ref, other, copies.reserve(1), mate)
+    block_copy.start()
 
     places = {"y": y, "z": z}
     rings = {"y": ring_y, "z": ring_z}
     orders = (("z", "y"), ("y", "z"))
-    share = width // STREAMS
-    half = share // 2
 
     class Stream:
         def __init__(self, index):
@@ -564,7 +562,17 @@
                 yield
             self.col_gather.finish()
 
+        def begin(self):
+            lanes = pl.ds(self.base, share)
+            for copy in start_copies[self.base // share]:
+                copy.wait_recv()
+            for q in range(4):
+                both = [start_land[2 * q, :, lanes], start_land[2 * q + 1, :, lanes]]
+                cols[q, self.all, :] = jnp.concatenate(both, axis=0).T
+            col_prev[self.all, :] = cols[x, self.all, :]
+
         def run(self):
+            self.begin()
             for step in range(3):
                 yield from self.to_rows()
                 yield from self.gather_rows(step)
@@ -574,55 +582,43 @@
                 self.scatters[colour][1].finish()
 
     streams = [Stream(index) for index in range(STREAMS)]
-    for stream in streams:
-        stream.col_gather.start()
-    local.wait()
-    prepare(block, core)
-    for stream in streams:
-        if stream.col_gather.relays:
-            stream.col_gather.forward()
-    start_copy.wait_send()
     block_copy.wait_recv()
     prepare(other, 1 - core)
     block_copy.wait_send()
-    for stream in streams:
-        stream.col_gather.finish()
 
     keep = pl.ds(pl.multiple_of(core * slab, slab), slab)
-    give = pl.ds(pl.multiple_of((1 - core) * slab, slab), slab)
-    top = pl.ds(0, slab)
     sums = [TotalSum(copies, (core, x, c), mate, peers, x_peers, buffers) for buffers in sum_buffers]
 
     def trade(piece, land, target):
         land[1] = piece.T
-        copy = copies.make(land.at[1, give, :], land.at[0, give, :], copies.reserve(1), mate)
+        copy = copies.make(land.at[1], land.at[0], copies.reserve(1), mate)
         copy.start()
         yield
         copy.wait()
-        target[:, mine_cols] = land[1, keep, :]
-        target[:, mate_cols] = land[0, keep, :]
+        target[:, mine_cols] = land[1]
+        target[:, mate_cols] = land[0]
 
     def first_chain():
         yield from trade(first_part[...], first_land, slab_ref)
-        sums[0].total[...] = contract(slab_ref[...], slab_ref[...], 0, 0)
+        sums[0].total[...] = contract(slab_ref[:, mine_cols], slab_ref[...], 0, 0)
         yield from sums[0].steps()
-        sums[0].total[...] = sums[0].result[...] / count
-        yield from factor_steps(2, sums[0].total, before_ref, tile, pend_left, pend_right)
+        sums[0].result[...] = sums[0].result[...] / count
+        yield from factor_steps(2, sums[0].result, before_ref, tile, pend_left, pend_right)
 
     def last_chain():
         yield from trade(col_prev[...], last_land, slab_ref)
         slab_ref[...] = contract(slab_ref[...], before_ref[...], 1, 1)
-        sums[1].total[...] = contract(slab_ref[...], slab_ref[...], 0, 0)
+        sums[1].total[...] = contract(slab_ref[:, mine_cols], slab_ref[...], 0, 0)
         yield from sums[1].steps()
-        sums[1].total[...] = sums[1].result[...] / count
-        yield from factor_steps(2, sums[1].total, inverse_ref, tile, pend_left, pend_right)
-        basis_ref[...] = contract(slab_ref[...], inverse_ref[...], 1, 1)
+        sums[1].result[...] = sums[1].result[...] / count
+        yield from factor_steps(2, sums[1].result, inverse_ref, tile, pend_left, pend_right)
+        basis_ref[...] = contract(slab_ref[keep, :], inverse_ref[...], 1, 1)
 
     def image_chain():
-        image_land[2, :, :] = row_parts[y, z].T
+        image_land[2] = row_parts[y, z].T
         slots = copies.reserve(2)
-        same = copies.make(image_land.at[2, keep, :], image_land.at[0, top, :], slots, device(z, core, y, x))
-        cross = copies.make(image_land.at[2, give, :], image_land.at[1, top, :], slots + 1, device(z, 1 - core, y, x))
+        same = copies.make(image_land.at[2], image_land.at[0], slots, device(z, core, y, x))
+        cross = copies.make(image_land.at[2], image_land.at[1], slots + 1, device(z, 1 - core, y, x))
         cross.start()
 
         @pl.when(crossed)
@@ -637,13 +633,13 @@
 
         @pl.when(jnp.logical_not(crossed))
         def _():
-            image_land[0, top, :] = image_land[2, keep, :]
+            image_land[0] = image_land[2]
 
         cross.wait()
-        image_ref[:, mine_cols] = image_land[0, top, :]
-        image_ref[:, mate_cols] = image_land[1, top, :]
+        image_ref[:, mine_cols] = image_land[0]
+        image_ref[:, mate_cols] = image_land[1]
         image_ref[...] = contract(image_ref[...], before_ref[...], 1, 1)
-        sums[2].total[...] = contract(slab_ref[...], image_ref[...], 0, 0)
+        sums[2].total[...] = contract(slab_ref[:, mine_cols], image_ref[...], 0, 0)
         yield from sums[2].steps()
 
     class Chain:
@@ -679,11 +675,14 @@
                 if chains[0].ended:
                     chains.pop(0)
 
+    for group in start_copies:
+        for copy in group:
+            copy.wait_send()
     inverse = inverse_ref[...]
     basis = basis_ref[...]
     projected = contract(product(inverse, sums[2].result[...] / count), inverse, 1, 1)
     projected_ref[...] = projected
-    residual_ref[...] = contract(image_ref[...], inverse, 1, 1) - product(basis, projected)
+    residual_ref[...] = contract(image_ref[keep, :], inverse, 1, 1) - product(basis, projected)
 
 
 def on_device(matrix, start_vectors, interval):
@@ -697,9 +696,8 @@
     tall = jax.ShapeDtypeStruct((slab, vectors), f32)
     square = jax.ShapeDtypeStruct((vectors, vectors), f32)
     one_sum = [
+        pltpu.VMEM((vectors // 2, vectors), f32),
         pltpu.VMEM((vectors, vectors), f32),
-        pltpu.VMEM((vectors, vectors), f32),
-        pltpu.VMEM((vectors // 2, vectors), f32),
         pltpu.VMEM((16, vectors // 32, vectors), f32),
         pltpu.VMEM((4, vectors // 32, vectors), f32),
     ]
@@ -724,12 +722,12 @@
             pltpu.VMEM((width, CHUNK), f32),
             pltpu.VMEM((width, CHUNK), f32),
             pltpu.VMEM((width, CHUNK), f32),
-            pltpu.VMEM((slab, width), f32),
+            pltpu.VMEM((8, slab, width), f32),
             pltpu.VMEM((2, CHUNK, width), f32),
             pltpu.VMEM((2, CHUNK, width), f32),
             pltpu.VMEM((3, CHUNK, width), f32),
-            pltpu.VMEM((slab, vectors), f32),
-            pltpu.VMEM((slab, vectors), f32),
+            pltpu.VMEM((CHUNK, vectors), f32),
+            pltpu.VMEM((CHUNK, vectors), f32),
             pltpu.VMEM((vectors, vectors), f32),
             pltpu.VMEM((vectors, vectors), f32),
             *(one_sum * 3),

time: 227 us -> 222 us (0.978)
  Pallas kernels: 221 us -> 216 us
    pallas_call x1, Pallas kernels: 221 us -> 216 us  [on_device(): pl.pallas_call(functools.partial(whole_kernel, total_rows), out_shape=(ta...]
where the time goes in v10:
time: 222 us
  Pallas kernels  216 us (97%)
  local copies, waits for them, and re-layouts  4.52 us (2%)
    pallas_call x1, Pallas kernels, on_device(): pl.pallas_call(functools.partial(whole_kernel, total_rows), out_shape=(ta...  216 us
    unnamed x5, local copies, waits for them, and re-layouts  4.52 us

profile of v10, /device:TPU:1, one launch (start us, length us, event | category | flops | bytes accessed | tf_op | source)
XLA Modules:
  0.0 221.6 jit_solution(10433652628497998258)
XLA Ops:
  0.6 216.4 %shard_map.58 = (f32[64,512]{1,0:T(8,128)}, f32[512,512]{1,0:T(8,128)}, f32[64,512]{1,0:T(8,128)}) custom-call(f32[2]{0:T(128)} %interval_ref.1, f32[1024,512]{1,0:T(8,128)} %block_ref.1, f32[64,512]{1,0:T(8,128)} %start_ref.1), custom_call_target="tpu_custom_call" | custom-call | flops 10000000000 | bytes 4000000 | tf_op jit(solution)/shard_map/pallas_call | solution.py:704
  217.1 0.0 copy-start
  217.1 1.6 copy.9
  218.7 2.3 %copy.10 = f32[512,512]{1,0:T(8,128)} copy(f32[512,512]{1,0:T(8,128)} %get-tuple-element.7) | data formatting | bytes 2097152
  221.0 0.0 copy-done
  221.0 0.7 copy.11
Async XLA Ops:
  217.1 3.9 %copy-start = (f32[64,512]{1,0:T(8,128)S(1)}, f32[64,512]{1,0:T(8,128)}, u32[]{:S(2)}) copy-start(f32[64,512]{1,0:T(8,128)} %get-tuple-element.8) | copy-start | bytes 393220

commit v11 on v10

--- a/solution.py
+++ b/solution.py
@@ -269,6 +269,10 @@
     count = left.shape[0] // 2
     both = one(left, right[0])
     return both[:count] + (both[count:] + one(left[:count], right[1]))
+
+
+def fine(left, right, right_dim):
+    return three_pass(jnp.concatenate(split(left), axis=0), split(right), ((1,), (right_dim,)))
 
 
 class TotalSum:
@@ -607,12 +611,12 @@
 
     def last_chain():
         yield from trade(col_prev[...], last_land, slab_ref)
-        slab_ref[...] = contract(slab_ref[...], before_ref[...], 1, 1)
+        slab_ref[...] = fine(slab_ref[...], before_ref[...], 1)
         sums[1].total[...] = contract(slab_ref[:, mine_cols], slab_ref[...], 0, 0)
         yield from sums[1].steps()
         sums[1].result[...] = sums[1].result[...] / count
         yield from factor_steps(2, sums[1].result, inverse_ref, tile, pend_left, pend_right)
-        basis_ref[...] = contract(slab_ref[keep, :], inverse_ref[...], 1, 1)
+        basis_ref[...] = fine(slab_ref[keep, :], inverse_ref[...], 1)
 
     def image_chain():
         image_land[2] = row_parts[y, z].T
@@ -638,7 +642,7 @@
         cross.wait()
         image_ref[:, mine_cols] = image_land[0]
         image_ref[:, mate_cols] = image_land[1]
-        image_ref[...] = contract(image_ref[...], before_ref[...], 1, 1)
+        image_ref[...] = fine(image_ref[...], before_ref[...], 1)
         sums[2].total[...] = contract(slab_ref[:, mine_cols], image_ref[...], 0, 0)
         yield from sums[2].steps()
 
@@ -656,7 +660,7 @@
     while not all(run.ended for run in runs):
         for index, run in enumerate(runs):
             run.advance()
-            if chains and (chains[0].ready or index == len(runs) - 1):
+            if chains and (begun == 1 and chains[0].ready or index == len(runs) - 1):
                 chains[0].advance()
                 if chains[0].ended:
                     chains.pop(0)
@@ -680,9 +684,9 @@
             copy.wait_send()
     inverse = inverse_ref[...]
     basis = basis_ref[...]
-    projected = contract(product(inverse, sums[2].result[...] / count), inverse, 1, 1)
+    projected = fine(fine(inverse, sums[2].result[...] / count, 0), inverse, 1)
     projected_ref[...] = projected
-    residual_ref[...] = contract(image_ref[keep, :], inverse, 1, 1) - product(basis, projected)
+    residual_ref[...] = fine(image_ref[keep, :], inverse, 1) - fine(basis, projected, 0)
 
 
 def on_device(matrix, start_vectors, interval):

time: 222 us -> 220 us (level)
    pallas_call x1, Pallas kernels: 216 us -> 214 us  [on_device(): pl.pallas_call(functools.partial(whole_kernel, total_rows), out_shape=(ta...]
where the time goes in v11:
time: 220 us; the launch traced here: 219 us
  Pallas kernels  214 us (97%)
  local copies, waits for them, and re-layouts  4.52 us (2%)
    pallas_call x1, Pallas kernels, on_device(): pl.pallas_call(functools.partial(whole_kernel, total_rows), out_shape=(ta...  214 us
    unnamed x5, local copies, waits for them, and re-layouts  4.52 us

profile of v11, /device:TPU:1, one launch (start us, length us, event | category | flops | bytes accessed | tf_op | source)
XLA Modules:
  0.0 219.3 jit_solution(2793218241176208261)
XLA Ops:
  0.6 214.1 %shard_map.58 = (f32[64,512]{1,0:T(8,128)}, f32[512,512]{1,0:T(8,128)}, f32[64,512]{1,0:T(8,128)}) custom-call(f32[2]{0:T(128)} %interval_ref.1, f32[1024,512]{1,0:T(8,128)} %block_ref.1, f32[64,512]{1,0:T(8,128)} %start_ref.1), custom_call_target="tpu_custom_call" | custom-call | flops 10000000000 | bytes 4000000 | tf_op jit(solution)/shard_map/pallas_call | solution.py:708
  214.8 0.0 copy-start
  214.8 1.6 copy.9
  216.4 2.3 %copy.10 = f32[512,512]{1,0:T(8,128)} copy(f32[512,512]{1,0:T(8,128)} %get-tuple-element.7) | data formatting | bytes 2097152
  218.6 0.0 copy-done
  218.6 0.7 copy.11
Async XLA Ops:
  214.8 3.9 %copy-start = (f32[64,512]{1,0:T(8,128)S(1)}, f32[64,512]{1,0:T(8,128)}, u32[]{:S(2)}) copy-start(f32[64,512]{1,0:T(8,128)} %get-tuple-element.8) | copy-start | bytes 393220

commit v12 on v11

--- a/solution.py
+++ b/solution.py
@@ -273,6 +273,12 @@
 
 def fine(left, right, right_dim):
     return three_pass(jnp.concatenate(split(left), axis=0), split(right), ((1,), (right_dim,)))
+
+
+def by_factor(left, inverse_ref):
+    half = inverse_ref.shape[0] // 2
+    first = fine(left[:, :half], inverse_ref[:half, :half], 1)
+    return jnp.concatenate([first, fine(left, inverse_ref[half:, :], 1)], axis=1)
 
 
 class TotalSum:
@@ -611,12 +617,12 @@
 
     def last_chain():
         yield from trade(col_prev[...], last_land, slab_ref)
-        slab_ref[...] = fine(slab_ref[...], before_ref[...], 1)
+        slab_ref[...] = by_factor(slab_ref[...], before_ref)
         sums[1].total[...] = contract(slab_ref[:, mine_cols], slab_ref[...], 0, 0)
         yield from sums[1].steps()
         sums[1].result[...] = sums[1].result[...] / count
         yield from factor_steps(2, sums[1].result, inverse_ref, tile, pend_left, pend_right)
-        basis_ref[...] = fine(slab_ref[keep, :], inverse_ref[...], 1)
+        basis_ref[...] = by_factor(slab_ref[keep, :], inverse_ref)
 
     def image_chain():
         image_land[2] = row_parts[y, z].T
@@ -642,7 +648,7 @@
         cross.wait()
         image_ref[:, mine_cols] = image_land[0]
         image_ref[:, mate_cols] = image_land[1]
-        image_ref[...] = fine(image_ref[...], before_ref[...], 1)
+        image_ref[...] = by_factor(image_ref[...], before_ref)
         sums[2].total[...] = contract(slab_ref[:, mine_cols], image_ref[...], 0, 0)
         yield from sums[2].steps()
 
@@ -684,9 +690,13 @@
             copy.wait_send()
     inverse = inverse_ref[...]
     basis = basis_ref[...]
-    projected = fine(fine(inverse, sums[2].result[...] / count, 0), inverse, 1)
+    cross = sums[2].result[...] / count
+    order = inverse.shape[0] // 2
+    upper = fine(inverse[:order, :order], cross[:order, :], 0)
+    lower = fine(inverse[order:, :], cross, 0)
+    projected = by_factor(jnp.concatenate([upper, lower], axis=0), inverse_ref)
     projected_ref[...] = projected
-    residual_ref[...] = fine(image_ref[keep, :], inverse, 1) - fine(basis, projected, 0)
+    residual_ref[...] = by_factor(image_ref[keep, :], inverse_ref) - fine(basis, projected, 0)
 
 
 def on_device(matrix, start_vectors, interval):

time: 220 us -> 218 us (level)
    pallas_call x1, Pallas kernels: 214 us -> 212 us  [on_device(): pl.pallas_call(functools.partial(whole_kernel, total_rows), out_shape=(ta...]
where the time goes in v12:
time: 218 us; the launch traced here: 217 us
  Pallas kernels  212 us (97%)
  local copies, waits for them, and re-layouts  4.52 us (2%)
    pallas_call x1, Pallas kernels, on_device(): pl.pallas_call(functools.partial(whole_kernel, total_rows), out_shape=(ta...  212 us
    unnamed x5, local copies, waits for them, and re-layouts  4.52 us

profile of v12, /device:TPU:1, one launch (start us, length us, event | category | flops | bytes accessed | tf_op | source)
XLA Modules:
  0.0 216.9 jit_solution(9389813984576311026)
XLA Ops:
  0.6 211.7 %shard_map.58 = (f32[64,512]{1,0:T(8,128)}, f32[512,512]{1,0:T(8,128)}, f32[64,512]{1,0:T(8,128)}) custom-call(f32[2]{0:T(128)} %interval_ref.1, f32[1024,512]{1,0:T(8,128)} %block_ref.1, f32[64,512]{1,0:T(8,128)} %start_ref.1), custom_call_target="tpu_custom_call" | custom-call | flops 10000000000 | bytes 4000000 | tf_op jit(solution)/shard_map/pallas_call | solution.py:718
  212.4 0.0 copy-start
  212.4 1.6 copy.9
  214.0 2.3 %copy.10 = f32[512,512]{1,0:T(8,128)} copy(f32[512,512]{1,0:T(8,128)} %get-tuple-element.7) | data formatting | bytes 2097152
  216.2 0.0 copy-done
  216.2 0.7 copy.11
Async XLA Ops:
  212.4 3.9 %copy-start = (f32[64,512]{1,0:T(8,128)S(1)}, f32[64,512]{1,0:T(8,128)}, u32[]{:S(2)}) copy-start(f32[64,512]{1,0:T(8,128)} %get-tuple-element.8) | copy-start | bytes 393220
